TPU v7x, 512 devices: a whole 4x8x8 slice. The times are simulated.
512 devices in a mesh: gx: 8 (over x, y_lo), gy: 8 (over y_hi, core), gz: 8 (over z).
Axes of the slice: x: 4, y: 8 (y_hi: 4, y_lo: 2; y = y_hi * 2 + y_lo), z: 8, core: 2. Of those that a mesh axis runs over, the one named last changes fastest.
Arguments:
- density: bfloat16 [8, 8, 8, 512, 256], P('gx', 'gy', 'gz'), may hold values from -6 to 6
- integrals: bfloat16 [8, 8, 8, 9, 512, 512], P('gx', 'gy', 'gz'), may hold values from -0.25 to 0.25
- offsets: int32 [8, 8, 8, 9], P('gx', 'gy', 'gz'), may hold values from 0 to 26, as said below
- counts: int32 [8, 8, 8], P('gx', 'gy', 'gz'), may hold values from 7 to 9, as said below
Outputs:
- exchange: bfloat16 [8, 8, 8, 512, 256], P('gx', 'gy', 'gz')
Inputs may be any that keep to these rules, and one draw needn't show every extreme that they name: Slots from counts[p] on hold no tile of domain p; some domain has all 9 slots live in every draw. `offsets`: a code names one of the 27 domains within one step along each axis, as the steps say; the 9 codes of one domain are all different.
All inputs are finite; a program needn't handle non-finite values.
Results may differ from a plain program's by a relative error of at most 0.006.
Values may be sent and summed in bfloat16 or wider, within the bound.
A program may use at most 64 MiB of HBM per device.

v0:
```python
import jax
import jax.numpy as jnp
from jax import lax
from jax.sharding import PartitionSpec as P


def extended_2(block, sides, width):
    for axis, dim in sides:
        count = lax.axis_size(axis)
        forward = [(i, i + 1) for i in range(count - 1)]
        forward.append((count - 1, 0))
        backward = [(target, source) for source, target in forward]
        low = lax.ppermute(
            lax.slice_in_dim(block, block.shape[dim] - width, None, axis=dim), axis, forward
        )
        high = lax.ppermute(lax.slice_in_dim(block, 0, width, axis=dim), axis, backward)
        block = jnp.concatenate([low, block, high], axis=dim)
    return block


def first_zdir(buffer):
    extended = extended_2(buffer, (("gz", 2),), 1)
    return (
        extended[:, :, 0:1].astype(jnp.float32)
        + extended[:, :, 2:3].astype(jnp.float32)
        + extended[:, :, 4:5].astype(jnp.float32)
    )


def collect_xdir(buffer):
    extended = extended_2(buffer.astype(jnp.bfloat16), (("gx", 0),), 1).astype(buffer.dtype)
    return extended[0:1] + extended[2:3] + extended[4:5]


def collect_ydir(buffer):
    extended = extended_2(buffer.astype(jnp.bfloat16), (("gy", 1),), 1).astype(buffer.dtype)
    return extended[:, 0:1] + extended[:, 2:3] + extended[:, 4:5]


def local(density, integrals, offsets, counts):
    block_rows = density.shape[3]
    columns = density.shape[4]
    slot_total = integrals.shape[3]
    own_block = density[0, 0, 0]
    tile_set = integrals[0, 0, 0]
    slot_codes = offsets[0, 0, 0]
    live_count = counts[0, 0, 0]
    extended = extended_2(density, (("gx", 0), ("gy", 1), ("gz", 2)), 1)
    neighbours = extended.reshape(27, block_rows, columns)
    slot_live = jnp.arange(slot_total, dtype=jnp.int32) < live_count
    selector = (
        (slot_codes[:, None] == jnp.arange(27, dtype=jnp.int32)[None, :]) & slot_live[:, None]
    ).astype(jnp.bfloat16)
    chosen = jnp.einsum(
        "so,obc->sbc", selector, neighbours, preferred_element_type=jnp.float32
    ).astype(jnp.bfloat16)
    forward = jnp.einsum("sij,sjc->ic", tile_set, chosen, preferred_element_type=jnp.float32)
    partial_value = jnp.einsum(
        "sji,jc->sic", tile_set, own_block, preferred_element_type=jnp.float32
    ).astype(jnp.bfloat16)
    outgoing = jnp.einsum(
        "so,sic->oic", selector, partial_value, preferred_element_type=jnp.float32
    ).astype(jnp.bfloat16)
    buffer = outgoing.reshape(3, 3, 3, block_rows, columns)
    buffer = collect_xdir(collect_ydir(first_zdir(buffer)))
    incoming = buffer[0, 0, 0]
    exchange = (forward + incoming).astype(jnp.bfloat16)
    return exchange[None, None, None]


def solution(mesh):
    return jax.shard_map(
        local,
        mesh=mesh,
        in_specs=(
            P("gx", "gy", "gz", None, None),
            P("gx", "gy", "gz", None, None, None),
            P("gx", "gy", "gz", None),
            P("gx", "gy", "gz"),
        ),
        out_specs=P("gx", "gy", "gz", None, None),
        check_vma=False,
    )
```

profile of v0, /device:TPU:1, one launch (start us, length us, event | category | flops | bytes accessed | tf_op | source)
XLA Modules:
  0.0 158.8 jit_solution(11811582316106428013)
XLA Ops:
  0.7 0.0 copy-start.1
  0.7 3.8 %fusion.2 = bf16[9,512,256]{2,1,0:T(8,128)(2,1)S(1)} fusion(bf16[1,1,1,9,512,512]{5,4,3,2,1,0:T(8,128)(2,1)} %param.5, bf16[1,1,1,512,256]{4,3,2,1,0:T(8,128)(2,1)} %param.4), kind=kOutput, calls=%fused_computation.5 | convolution fusion | flops 1207959552 | bytes 7340032 | tf_op jit(solution)/shard_map/sji,jc->sic/dot_general | solution.py:58
  4.5 0.0 copy-done.1
  4.5 5.3 %convolution_convert_fusion = bf16[27,512,256]{2,0,1:T(8,128)(2,1)} fusion(bf16[9,512,256]{2,1,0:T(8,128)(2,1)S(1)} %fusion.2, s32[9]{0:T(128)S(1)} %bitcast.43, pred[9]{0:T(512)(128)(4,1)S(1)} %iota_compare_fusion.1), kind=kOutput, calls=%fused_computation.4 | convolution fusion | flops 67240424 | bytes 9437229 | tf_op jit(solution)/shard_map/so,sic->oic/dot_general | solution.py:61
  9.8 13.6 %copy.5 = bf16[27,512,256]{1,2,0:T(8,128)(2,1)} copy(bf16[27,512,256]{2,0,1:T(8,128)(2,1)} %convolution_convert_fusion) | data formatting | bytes 14155776 | tf_op jit(solution)/shard_map/convert_element_type | solution.py:63
  23.4 0.0 copy-start
  23.4 2.8 %fusion.28 = (bf16[3,3,1,512,256]{3,4,2,1,0:T(8,128)(2,1)S(1)}, bf16[3,3,1,512,256]{3,4,2,1,0:T(8,128)(2,1)S(1)}) fusion(bf16[3,3,3,512,256]{3,4,2,1,0:T(8,128)(2,1)} %bitcast.41), kind=kLoop, calls=%fused_computation.38 | loop fusion | bytes 9437184 | tf_op jit(solution)/shard_map/slice | solution.py:14
  26.3 4.8 %collective-permute-start.6 = (bf16[3,3,1,512,256]{3,4,2,1,0:T(8,128)(2,1)S(1)}, bf16[3,3,1,512,256]{3,4,2,1,0:T(8,128)(2,1)S(1)}, u32[]{:S(2)}, u32[]{:S(2)}) collective-permute-start(bf16[3,3,1,512,256]{3,4,2,1,0:T(8,128)(2,1)S(1)} %get-tuple-element.5), channel_id=1, source_target_pairs={{0,1},{1,2},{2,3},{3,4},{4,5},{5,6},{6,7},{7,0},{8,9},{9,10},{10,1... | collective-permute-start | bytes 7077896 | tf_op jit(solution)/shard_map/ppermute | solution.py:13
  31.1 8.6 %collective-permute-start.7 = (bf16[3,3,1,512,256]{3,4,2,1,0:T(8,128)(2,1)S(1)}, bf16[3,3,1,512,256]{3,4,2,1,0:T(8,128)(2,1)S(1)}, u32[]{:S(2)}, u32[]{:S(2)}) collective-permute-start(bf16[3,3,1,512,256]{3,4,2,1,0:T(8,128)(2,1)S(1)} %get-tuple-element.6), channel_id=1, source_target_pairs={{1,0},{2,1},{3,2},{4,3},{5,4},{6,5},{7,6},{0,7},{9,8},{10,9},{11,1... | collective-permute-start | bytes 7077896 | tf_op jit(solution)/shard_map/ppermute | solution.py:16
  39.7 0.0 copy-done
  39.7 3.2 %collective-permute-start = (bf16[1,1,1,512,256]{4,3,2,1,0:T(8,128)(2,1)S(1)}, bf16[1,1,1,512,256]{4,3,2,1,0:T(8,128)(2,1)S(1)}, u32[]{:S(2)}, u32[]{:S(2)}) collective-permute-start(bf16[1,1,1,512,256]{4,3,2,1,0:T(8,128)(2,1)S(1)} %copy-done), channel_id=1, source_target_pairs={{0,64},{64,128},{128,192},{192,256},{256,320},{320,384},{384,448},... | collective-permute-start | bytes 786440 | tf_op jit(solution)/shard_map/ppermute | solution.py:13
  42.9 4.2 %collective-permute-start.1 = (bf16[1,1,1,512,256]{4,3,2,1,0:T(8,128)(2,1)S(1)}, bf16[1,1,1,512,256]{4,3,2,1,0:T(8,128)(2,1)S(1)}, u32[]{:S(2)}, u32[]{:S(2)}) collective-permute-start(bf16[1,1,1,512,256]{4,3,2,1,0:T(8,128)(2,1)S(1)} %copy-done), channel_id=1, source_target_pairs={{64,0},{128,64},{192,128},{256,192},{320,256},{384,320},{448,384},... | collective-permute-start | bytes 786440 | tf_op jit(solution)/shard_map/ppermute | solution.py:16
  47.1 3.5 %collective-permute-done = bf16[1,1,1,512,256]{4,3,2,1,0:T(8,128)(2,1)S(1)} collective-permute-done((bf16[1,1,1,512,256]{4,3,2,1,0:T(8,128)(2,1)S(1)}, bf16[1,1,1,512,256]{4,3,2,1,0:T(8,128)(2,1)S(1)}, u32[]{:S(2)}, u32[]{:S(2)}) %collective-permute-start) | collective-permute-done | bytes 262176 | tf_op jit(solution)/shard_map/ppermute | solution.py:13
  50.7 4.4 %collective-permute-done.1 = bf16[1,1,1,512,256]{4,3,2,1,0:T(8,128)(2,1)S(1)} collective-permute-done((bf16[1,1,1,512,256]{4,3,2,1,0:T(8,128)(2,1)S(1)}, bf16[1,1,1,512,256]{4,3,2,1,0:T(8,128)(2,1)S(1)}, u32[]{:S(2)}, u32[]{:S(2)}) %collective-permute-start.1) | collective-permute-done | bytes 262176 | tf_op jit(solution)/shard_map/ppermute | solution.py:16
  55.1 5.9 %collective-permute-start.2 = (bf16[3,1,1,512,256]{4,3,2,1,0:T(8,128)(2,1)S(1)}, bf16[3,1,1,512,256]{4,3,2,1,0:T(8,128)(2,1)S(1)}, u32[]{:S(2)}, u32[]{:S(2)}) collective-permute-start(bf16[3,1,1,512,256]{4,3,2,1,0:T(8,128)(2,1)S(1)} %constant_dynamic-update-slice_fusion), channel_id=1, source_target_pairs={{0,8},{8,16},{16,24},{24,32},{32,40},{40,48},{48,56},{56,0},{1,9},... | collective-permute-start | bytes 2359304 | tf_op jit(solution)/shard_map/ppermute | solution.py:13
  61.0 1.9 %collective-permute-start.3 = (bf16[3,1,1,512,256]{4,3,2,1,0:T(8,128)(2,1)S(1)}, bf16[3,1,1,512,256]{4,3,2,1,0:T(8,128)(2,1)S(1)}, u32[]{:S(2)}, u32[]{:S(2)}) collective-permute-start(bf16[3,1,1,512,256]{4,3,2,1,0:T(8,128)(2,1)S(1)} %constant_dynamic-update-slice_fusion), channel_id=1, source_target_pairs={{8,0},{16,8},{24,16},{32,24},{40,32},{48,40},{56,48},{0,56},{9,1},... | collective-permute-start | bytes 2359304 | tf_op jit(solution)/shard_map/ppermute | solution.py:16
  62.9 10.9 %collective-permute-done.2 = bf16[3,1,1,512,256]{4,3,2,1,0:T(8,128)(2,1)S(1)} collective-permute-done((bf16[3,1,1,512,256]{4,3,2,1,0:T(8,128)(2,1)S(1)}, bf16[3,1,1,512,256]{4,3,2,1,0:T(8,128)(2,1)S(1)}, u32[]{:S(2)}, u32[]{:S(2)}) %collective-permute-start.2) | collective-permute-done | bytes 786464 | tf_op jit(solution)/shard_map/ppermute | solution.py:13
  73.8 10.2 %collective-permute-done.3 = bf16[3,1,1,512,256]{4,3,2,1,0:T(8,128)(2,1)S(1)} collective-permute-done((bf16[3,1,1,512,256]{4,3,2,1,0:T(8,128)(2,1)S(1)}, bf16[3,1,1,512,256]{4,3,2,1,0:T(8,128)(2,1)S(1)}, u32[]{:S(2)}, u32[]{:S(2)}) %collective-permute-start.3) | collective-permute-done | bytes 786464 | tf_op jit(solution)/shard_map/ppermute | solution.py:16
  84.0 0.3 pad_maximum_fusion.1
  84.2 1.9 %collective-permute-start.4 = (bf16[3,3,1,512,256]{4,3,2,1,0:T(8,128)(2,1)S(1)}, bf16[3,3,1,512,256]{4,3,2,1,0:T(8,128)(2,1)S(1)}, u32[]{:S(2)}, u32[]{:S(2)}) collective-permute-start(bf16[3,3,1,512,256]{4,3,2,1,0:T(8,128)(2,1)S(1)} %pad_maximum_fusion.1), channel_id=1, source_target_pairs={{0,1},{1,2},{2,3},{3,4},{4,5},{5,6},{6,7},{7,0},{8,9},{9,10},{10,1... | collective-permute-start | bytes 7077896 | tf_op jit(solution)/shard_map/ppermute | solution.py:13
  86.1 4.6 %collective-permute-start.5 = (bf16[3,3,1,512,256]{4,3,2,1,0:T(8,128)(2,1)S(1)}, bf16[3,3,1,512,256]{4,3,2,1,0:T(8,128)(2,1)S(1)}, u32[]{:S(2)}, u32[]{:S(2)}) collective-permute-start(bf16[3,3,1,512,256]{4,3,2,1,0:T(8,128)(2,1)S(1)} %pad_maximum_fusion.1), channel_id=1, source_target_pairs={{1,0},{2,1},{3,2},{4,3},{5,4},{6,5},{7,6},{0,7},{9,8},{10,9},{11,1... | collective-permute-start | bytes 7077896 | tf_op jit(solution)/shard_map/ppermute | solution.py:16
  90.7 0.0 collective-permute-done.6
  90.7 0.0 collective-permute-done.7
  90.8 2.7 %add_convert_fusion = bf16[3,3,1,512,256]{3,4,2,1,0:T(8,128)(2,1)S(1)} fusion(bf16[3,3,1,512,256]{3,4,2,1,0:T(8,128)(2,1)S(1)} %collective-permute-done.7, bf16[3,3,1,512,256]{3,4,2,1,0:T(8,128)(2,1)S(1)} %collective-permute-done.6, bf16[3,3,3,512,256]{3,4,2,1,0:T(8,128)(2,1)} %bitcast.42), kind=kLoop, calls=%fused_computation.9 | loop fusion | flops 7077888 | bytes 9437184 | tf_op jit(solution)/shard_map/convert_element_type | solution.py:36
  93.4 0.2 fusion.29
  93.6 4.5 %collective-permute-start.8 = (bf16[3,1,1,512,256]{3,4,2,1,0:T(8,128)(2,1)S(1)}, bf16[3,1,1,512,256]{3,4,2,1,0:T(8,128)(2,1)S(1)}, u32[]{:S(2)}, u32[]{:S(2)}) collective-permute-start(bf16[3,1,1,512,256]{3,4,2,1,0:T(8,128)(2,1)S(1)} %get-tuple-element.7), channel_id=1, source_target_pairs={{0,8},{8,16},{16,24},{24,32},{32,40},{40,48},{48,56},{56,0},{1,9},... | collective-permute-start | bytes 2359304 | tf_op jit(solution)/shard_map/ppermute | solution.py:13
  98.1 1.9 %collective-permute-start.9 = (bf16[3,1,1,512,256]{3,4,2,1,0:T(8,128)(2,1)S(1)}, bf16[3,1,1,512,256]{3,4,2,1,0:T(8,128)(2,1)S(1)}, u32[]{:S(2)}, u32[]{:S(2)}) collective-permute-start(bf16[3,1,1,512,256]{3,4,2,1,0:T(8,128)(2,1)S(1)} %get-tuple-element.8), channel_id=1, source_target_pairs={{8,0},{16,8},{24,16},{32,24},{40,32},{48,40},{56,48},{0,56},{9,1},... | collective-permute-start | bytes 2359304 | tf_op jit(solution)/shard_map/ppermute | solution.py:16
  100.0 9.8 %collective-permute-done.8 = bf16[3,1,1,512,256]{3,4,2,1,0:T(8,128)(2,1)S(1)} collective-permute-done((bf16[3,1,1,512,256]{3,4,2,1,0:T(8,128)(2,1)S(1)}, bf16[3,1,1,512,256]{3,4,2,1,0:T(8,128)(2,1)S(1)}, u32[]{:S(2)}, u32[]{:S(2)}) %collective-permute-start.8) | collective-permute-done | bytes 786464 | tf_op jit(solution)/shard_map/ppermute | solution.py:13
  109.9 11.2 %collective-permute-done.9 = bf16[3,1,1,512,256]{3,4,2,1,0:T(8,128)(2,1)S(1)} collective-permute-done((bf16[3,1,1,512,256]{3,4,2,1,0:T(8,128)(2,1)S(1)}, bf16[3,1,1,512,256]{3,4,2,1,0:T(8,128)(2,1)S(1)}, u32[]{:S(2)}, u32[]{:S(2)}) %collective-permute-start.9) | collective-permute-done | bytes 786464 | tf_op jit(solution)/shard_map/ppermute | solution.py:16
  121.1 0.4 fusion.8
  121.5 0.7 fusion.30
  122.2 1.9 %collective-permute-start.10 = (bf16[1,1,1,512,256]{3,4,2,1,0:T(8,128)(2,1)}, bf16[1,1,1,512,256]{3,4,2,1,0:T(8,128)(2,1)}, u32[]{:S(2)}, u32[]{:S(2)}) collective-permute-start(bf16[1,1,1,512,256]{3,4,2,1,0:T(8,128)(2,1)} %get-tuple-element.9), channel_id=1, source_target_pairs={{0,64},{64,128},{128,192},{192,256},{256,320},{320,384},{384,448},... | collective-permute-start | bytes 786440 | tf_op jit(solution)/shard_map/ppermute | solution.py:13
  124.1 5.7 %collective-permute-start.11 = (bf16[1,1,1,512,256]{3,4,2,1,0:T(8,128)(2,1)S(1)}, bf16[1,1,1,512,256]{3,4,2,1,0:T(8,128)(2,1)}, u32[]{:S(2)}, u32[]{:S(2)}) collective-permute-start(bf16[1,1,1,512,256]{3,4,2,1,0:T(8,128)(2,1)S(1)} %get-tuple-element.10), channel_id=1, source_target_pairs={{64,0},{128,64},{192,128},{256,192},{320,256},{384,320},{448,384},... | collective-permute-start | bytes 786440 | tf_op jit(solution)/shard_map/ppermute | solution.py:16
  129.8 10.0 %collective-permute-done.4 = bf16[3,3,1,512,256]{4,3,2,1,0:T(8,128)(2,1)S(1)} collective-permute-done((bf16[3,3,1,512,256]{4,3,2,1,0:T(8,128)(2,1)S(1)}, bf16[3,3,1,512,256]{4,3,2,1,0:T(8,128)(2,1)S(1)}, u32[]{:S(2)}, u32[]{:S(2)}) %collective-permute-start.4) | collective-permute-done | bytes 2359328 | tf_op jit(solution)/shard_map/ppermute | solution.py:13
  139.8 1.5 collective-permute-done.5
  141.3 0.8 pad_maximum_fusion
  142.1 6.0 %fusion = bf16[9,512,256]{2,0,1:T(8,128)(2,1)} fusion(bf16[27,512,256]{2,1,0:T(8,128)(2,1)S(1)} %bitcast.40, s32[9]{0:T(128)S(1)} %bitcast.44, pred[9]{0:T(512)(128)(4,1)S(1)} %iota_compare_fusion.1), kind=kOutput, calls=%fused_computation.1 | convolution fusion | flops 63701480 | bytes 9437229 | tf_op jit(solution)/shard_map/so,obc->sbc/dot_general | solution.py:54
  148.1 5.9 %copy.8 = bf16[9,512,256]{1,2,0:T(8,128)(2,1)S(1)} copy(bf16[9,512,256]{2,0,1:T(8,128)(2,1)} %fusion) | data formatting | bytes 4718592 | tf_op jit(solution)/shard_map/so,obc->sbc/dot_general | solution.py:54
  154.0 0.0 collective-permute-done.10
  154.1 0.0 collective-permute-done.11
  154.1 3.9 %fusion.18 = bf16[1,1,1,512,256]{3,4,2,1,0:T(8,128)(2,1)S(1)} fusion(bf16[1,1,1,512,256]{3,4,2,1,0:T(8,128)(2,1)} %collective-permute-done.11, bf16[3,1,1,512,256]{3,4,2,1,0:T(8,128)(2,1)S(1)} %fusion.8, bf16[1,1,1,512,256]{3,4,2,1,0:T(8,128)(2,1)} %collective-permute-done.10, bf16[9,512,256]{1,2,0:T(8,128)(2,1)S(1)} %copy.8, ...), kind=kOutput, calls=%fused_computation.23 | convolution fusion | flops 1209663488 | bytes 8650752 | tf_op jit(solution)/shard_map/sij,sjc->ic/dot_general | solution.py:57
  157.9 0.8 copy.6
  (4 shorter events, 0.1 us)
Async XLA Ops:
  0.7 3.8 %copy-start.1 = (s32[1,1,1,9]{3,2,1,0:T(1,128)S(1)}, s32[1,1,1,9]{3,2,1,0:T(1,128)}, u32[]{:S(2)}) copy-start(s32[1,1,1,9]{3,2,1,0:T(1,128)} %param.6) | copy-start | bytes 112
  23.4 16.3 %copy-start = (bf16[1,1,1,512,256]{4,3,2,1,0:T(8,128)(2,1)S(1)}, bf16[1,1,1,512,256]{4,3,2,1,0:T(8,128)(2,1)}, u32[]{:S(2)}) copy-start(bf16[1,1,1,512,256]{4,3,2,1,0:T(8,128)(2,1)} %param.4) | copy-start | bytes 786436
  26.3 64.5 %collective-permute-start.6 = (bf16[3,3,1,512,256]{3,4,2,1,0:T(8,128)(2,1)S(1)}, bf16[3,3,1,512,256]{3,4,2,1,0:T(8,128)(2,1)S(1)}, u32[]{:S(2)}, u32[]{:S(2)}) collective-permute-start(bf16[3,3,1,512,256]{3,4,2,1,0:T(8,128)(2,1)S(1)} %get-tuple-element.5), channel_id=1, source_target_pairs={{0,1},{1,2},{2,3},{3,4},{4,5},{5,6},{6,7},{7,0},{8,9},{9,10},{10,1... | collective-permute-start | bytes 7077896 | tf_op jit(solution)/shard_map/ppermute | solution.py:13
  31.1 59.7 %collective-permute-start.7 = (bf16[3,3,1,512,256]{3,4,2,1,0:T(8,128)(2,1)S(1)}, bf16[3,3,1,512,256]{3,4,2,1,0:T(8,128)(2,1)S(1)}, u32[]{:S(2)}, u32[]{:S(2)}) collective-permute-start(bf16[3,3,1,512,256]{3,4,2,1,0:T(8,128)(2,1)S(1)} %get-tuple-element.6), channel_id=1, source_target_pairs={{1,0},{2,1},{3,2},{4,3},{5,4},{6,5},{7,6},{0,7},{9,8},{10,9},{11,1... | collective-permute-start | bytes 7077896 | tf_op jit(solution)/shard_map/ppermute | solution.py:16
  39.7 10.9 %collective-permute-start = (bf16[1,1,1,512,256]{4,3,2,1,0:T(8,128)(2,1)S(1)}, bf16[1,1,1,512,256]{4,3,2,1,0:T(8,128)(2,1)S(1)}, u32[]{:S(2)}, u32[]{:S(2)}) collective-permute-start(bf16[1,1,1,512,256]{4,3,2,1,0:T(8,128)(2,1)S(1)} %copy-done), channel_id=1, source_target_pairs={{0,64},{64,128},{128,192},{192,256},{256,320},{320,384},{384,448},... | collective-permute-start | bytes 786440 | tf_op jit(solution)/shard_map/ppermute | solution.py:13
  42.9 12.1 %collective-permute-start.1 = (bf16[1,1,1,512,256]{4,3,2,1,0:T(8,128)(2,1)S(1)}, bf16[1,1,1,512,256]{4,3,2,1,0:T(8,128)(2,1)S(1)}, u32[]{:S(2)}, u32[]{:S(2)}) collective-permute-start(bf16[1,1,1,512,256]{4,3,2,1,0:T(8,128)(2,1)S(1)} %copy-done), channel_id=1, source_target_pairs={{64,0},{128,64},{192,128},{256,192},{320,256},{384,320},{448,384},... | collective-permute-start | bytes 786440 | tf_op jit(solution)/shard_map/ppermute | solution.py:16
  55.1 18.7 %collective-permute-start.2 = (bf16[3,1,1,512,256]{4,3,2,1,0:T(8,128)(2,1)S(1)}, bf16[3,1,1,512,256]{4,3,2,1,0:T(8,128)(2,1)S(1)}, u32[]{:S(2)}, u32[]{:S(2)}) collective-permute-start(bf16[3,1,1,512,256]{4,3,2,1,0:T(8,128)(2,1)S(1)} %constant_dynamic-update-slice_fusion), channel_id=1, source_target_pairs={{0,8},{8,16},{16,24},{24,32},{32,40},{40,48},{48,56},{56,0},{1,9},... | collective-permute-start | bytes 2359304 | tf_op jit(solution)/shard_map/ppermute | solution.py:13
  61.0 23.0 %collective-permute-start.3 = (bf16[3,1,1,512,256]{4,3,2,1,0:T(8,128)(2,1)S(1)}, bf16[3,1,1,512,256]{4,3,2,1,0:T(8,128)(2,1)S(1)}, u32[]{:S(2)}, u32[]{:S(2)}) collective-permute-start(bf16[3,1,1,512,256]{4,3,2,1,0:T(8,128)(2,1)S(1)} %constant_dynamic-update-slice_fusion), channel_id=1, source_target_pairs={{8,0},{16,8},{24,16},{32,24},{40,32},{48,40},{56,48},{0,56},{9,1},... | collective-permute-start | bytes 2359304 | tf_op jit(solution)/shard_map/ppermute | solution.py:16
  84.2 55.6 %collective-permute-start.4 = (bf16[3,3,1,512,256]{4,3,2,1,0:T(8,128)(2,1)S(1)}, bf16[3,3,1,512,256]{4,3,2,1,0:T(8,128)(2,1)S(1)}, u32[]{:S(2)}, u32[]{:S(2)}) collective-permute-start(bf16[3,3,1,512,256]{4,3,2,1,0:T(8,128)(2,1)S(1)} %pad_maximum_fusion.1), channel_id=1, source_target_pairs={{0,1},{1,2},{2,3},{3,4},{4,5},{5,6},{6,7},{7,0},{8,9},{9,10},{10,1... | collective-permute-start | bytes 7077896 | tf_op jit(solution)/shard_map/ppermute | solution.py:13
  86.1 55.1 %collective-permute-start.5 = (bf16[3,3,1,512,256]{4,3,2,1,0:T(8,128)(2,1)S(1)}, bf16[3,3,1,512,256]{4,3,2,1,0:T(8,128)(2,1)S(1)}, u32[]{:S(2)}, u32[]{:S(2)}) collective-permute-start(bf16[3,3,1,512,256]{4,3,2,1,0:T(8,128)(2,1)S(1)} %pad_maximum_fusion.1), channel_id=1, source_target_pairs={{1,0},{2,1},{3,2},{4,3},{5,4},{6,5},{7,6},{0,7},{9,8},{10,9},{11,1... | collective-permute-start | bytes 7077896 | tf_op jit(solution)/shard_map/ppermute | solution.py:16
  93.6 16.2 %collective-permute-start.8 = (bf16[3,1,1,512,256]{3,4,2,1,0:T(8,128)(2,1)S(1)}, bf16[3,1,1,512,256]{3,4,2,1,0:T(8,128)(2,1)S(1)}, u32[]{:S(2)}, u32[]{:S(2)}) collective-permute-start(bf16[3,1,1,512,256]{3,4,2,1,0:T(8,128)(2,1)S(1)} %get-tuple-element.7), channel_id=1, source_target_pairs={{0,8},{8,16},{16,24},{24,32},{32,40},{40,48},{48,56},{56,0},{1,9},... | collective-permute-start | bytes 2359304 | tf_op jit(solution)/shard_map/ppermute | solution.py:13
  98.1 23.0 %collective-permute-start.9 = (bf16[3,1,1,512,256]{3,4,2,1,0:T(8,128)(2,1)S(1)}, bf16[3,1,1,512,256]{3,4,2,1,0:T(8,128)(2,1)S(1)}, u32[]{:S(2)}, u32[]{:S(2)}) collective-permute-start(bf16[3,1,1,512,256]{3,4,2,1,0:T(8,128)(2,1)S(1)} %get-tuple-element.8), channel_id=1, source_target_pairs={{8,0},{16,8},{24,16},{32,24},{40,32},{48,40},{56,48},{0,56},{9,1},... | collective-permute-start | bytes 2359304 | tf_op jit(solution)/shard_map/ppermute | solution.py:16
  122.2 31.8 %collective-permute-start.10 = (bf16[1,1,1,512,256]{3,4,2,1,0:T(8,128)(2,1)}, bf16[1,1,1,512,256]{3,4,2,1,0:T(8,128)(2,1)}, u32[]{:S(2)}, u32[]{:S(2)}) collective-permute-start(bf16[1,1,1,512,256]{3,4,2,1,0:T(8,128)(2,1)} %get-tuple-element.9), channel_id=1, source_target_pairs={{0,64},{64,128},{128,192},{192,256},{256,320},{320,384},{384,448},... | collective-permute-start | bytes 786440 | tf_op jit(solution)/shard_map/ppermute | solution.py:13
  124.1 29.9 %collective-permute-start.11 = (bf16[1,1,1,512,256]{3,4,2,1,0:T(8,128)(2,1)S(1)}, bf16[1,1,1,512,256]{3,4,2,1,0:T(8,128)(2,1)}, u32[]{:S(2)}, u32[]{:S(2)}) collective-permute-start(bf16[1,1,1,512,256]{3,4,2,1,0:T(8,128)(2,1)S(1)} %get-tuple-element.10), channel_id=1, source_target_pairs={{64,0},{128,64},{192,128},{256,192},{320,256},{384,320},{448,384},... | collective-permute-start | bytes 786440 | tf_op jit(solution)/shard_map/ppermute | solution.py:16
where the time goes:
time: 160 us; the launch traced here: 159 us
  waiting for transfers between devices  61.5 us (38%)
  starting transfers between devices  49.1 us (31%)
  local copies, waits for them, and re-layouts  24.2 us (15%)
  matrix products  18.9 us (12%)
  other arithmetic  4.19 us (3%)
    ppermute x6, waiting for transfers between devices, extended_2(): lax.ppermute(lax.slice_in_dim(block, block.shape[dim] - width, None, axis...  34.2 us
    ppermute x6, waiting for transfers between devices, extended_2(): lax.ppermute(lax.slice_in_dim(block, 0, width, axis=dim), axis, backward)  27.3 us
    ppermute x6, starting transfers between devices, extended_2(): lax.ppermute(lax.slice_in_dim(block, 0, width, axis=dim), axis, backward)  26.8 us
    ppermute x6, starting transfers between devices, extended_2(): lax.ppermute(lax.slice_in_dim(block, block.shape[dim] - width, None, axis...  22.2 us
    convert_element_type x1, local copies, waits for them, and re-layouts, local(): outgoing = jnp.einsum('so,sic->oic', selector, partial_value, preferred_e...  13.6 us
    dot_general x1, matrix products, local(): jnp.einsum('so,obc->sbc', selector, neighbours, preferred_element_type=jn...  5.99 us
    dot_general x1, local copies, waits for them, and re-layouts, local(): jnp.einsum('so,obc->sbc', selector, neighbours, preferred_element_type=jn...  5.91 us
    dot_general x1, matrix products, local(): jnp.einsum('so,sic->oic', selector, partial_value, preferred_element_type...  5.27 us
  transfers between devices with their start and end apart: 12, of which 8 were waited for; matrix products, arithmetic and copies ran while one was open for 11% of the time, Pallas kernels for 0%

commit v1 on v0

v1 whole, which is shorter than its diff:
```python
import functools

import jax
import jax.numpy as jnp
from jax import lax
from jax.experimental import pallas as pl
from jax.experimental.pallas import tpu as pltpu
from jax.sharding import PartitionSpec as P

MESH = pl.DeviceIdType.MESH
OWN, PAR, CRS = 0, 1, 2
CHUNKS = 2
ORDER = (
    0, 1, 30, 31, 32, 33, 34, 35, 36, 37, 38, 2, 3, 5, 39, 40, 41, 42, 43, 44, 45, 46, 47, 48, 53, 55, 68, 70,
    16, 17, 19, 52, 49, 10, 50, 51, 64, 65, 8, 66, 4, 6, 67, 13, 54, 22, 69, 18, 7, 20, 24, 9, 59, 27, 14, 56,
    11, 74, 58, 15, 71, 21, 28, 12, 61, 60, 57, 23, 29, 72, 25, 76, 26, 73, 62, 75, 79, 63, 77, 78,
)


def slot(group, dz, k):
    return ("H", group * 9 + dz * 3 + k)


def far(dz, k):
    return ("F", dz * 2 + k)


def out_slot(group, dz, k):
    return ("O", (group - 1) * 9 + dz * 3 + k)


class Task:
    def __init__(self, kind, q, waits=(), waits_s=(), waits_r=(), sends=(), cost=0.0, args=()):
        self.kind = kind
        self.q = q
        self.waits = list(waits)
        self.waits_s = list(waits_s)
        self.waits_r = list(waits_r)
        self.sends = list(sends)
        self.cost = cost
        self.args = args


def make_tasks(chunks):
    tasks = []
    for q in range(chunks):
        c = slot(0, 1, OWN)
        tasks.append(Task("relay", q, sends=[
            (c, slot(0, 1, PAR), "partner", None),
            (c, slot(0, 0, OWN), "zp", None),
            (c, slot(0, 2, OWN), "zm", None),
            (c, far(1, PAR), "outer", "S"),
            (c, slot(1, 1, OWN), "sib", None),
        ]))
    for q in range(chunks):
        c = slot(0, 1, PAR)
        tasks.append(Task("relay", q, [c], sends=[
            (c, slot(0, 1, CRS), "xd", None),
            (c, far(1, OWN), "outer", "S"),
            (c, slot(0, 0, PAR), "zp", None),
            (c, slot(0, 2, PAR), "zm", None),
            (c, slot(1, 1, PAR), "sib", None),
        ]))
        for dz in (0, 2):
            c = slot(0, dz, OWN)
            tasks.append(Task("relay", q, [c], sends=[
                (c, far(dz, PAR), "outer", "S"),
                (c, slot(1, dz, OWN), "sib", None),
            ]))
            c = slot(0, dz, PAR)
            tasks.append(Task("relay", q, [c], sends=[
                (c, far(dz, OWN), "outer", "S"),
                (c, slot(0, dz, CRS), "xd", None),
                (c, slot(1, dz, PAR), "sib", None),
            ]))
        for dz in (0, 1, 2):
            c = slot(0, dz, CRS)
            tasks.append(Task("relay", q, [c], sends=[(c, slot(1, dz, CRS), "sib", None)]))
        for k in (OWN, PAR):
            for dz in (1, 0, 2):
                c = far(dz, k)
                sends = []
                if dz == 1:
                    sends += [
                        (c, far(1, 1 - k), "partner", "R"),
                        (c, far(0, k), "zp", "S"),
                        (c, far(2, k), "zm", "S"),
                    ]
                if k == PAR:
                    sends.append((c, slot(2, dz, CRS), "sxd", None))
                sends.append((c, slot(2, dz, k), "sib", None))
                tasks.append(Task("relay", q, [c], sends=sends))
    tasks.append(Task("part", None, cost=3.5))
    for dz in (0, 2, 1):
        tasks.append(Task("sel", None, cost=0.12, args=(2, dz, CRS), sends=[
            (out_slot(2, dz, CRS), ("XF", dz), "sxp", None)]))
        for k in (PAR, OWN):
            tasks.append(Task("sel", None, cost=0.12, args=(2, dz, k), sends=[
                (out_slot(2, dz, k), ("RF", dz * 2 + k), "sib", None)]))
    for k in (CRS, PAR, OWN):
        for dz in (0, 2, 1):
            tasks.append(Task("sel", None, cost=0.12, args=(1, dz, k), sends=[
                (out_slot(1, dz, k), ("RN", dz * 3 + k), "sib", None)]))
    unit = 0.6 / chunks
    for q in range(chunks):
        for dz in (0, 2, 1):
            tasks.append(Task("cross", q, [("RN", dz * 3 + CRS)], cost=unit, args=(dz,), sends=[
                (("AX", dz), ("XN", dz), "xp", None)]))
        for dz in (0, 2):
            for k in (PAR, OWN):
                waits = [("RF", dz * 2 + k)]
                source = ("RF", dz * 2 + k)
                if k == PAR:
                    waits.append(("XF", dz))
                    source = ("AF", dz * 2 + k)
                tasks.append(Task("farz" if k == PAR else "relay", q, waits, cost=unit if k == PAR else 0.0,
                                  args=(dz,), sends=[
                    (source, ("ZF", (0 if dz == 0 else 2) + k), "zm" if dz == 0 else "zp", "S"),
                    (source, ("EN", dz * 2 + 1 - k), "outer", "R")]))
        for k in (PAR, OWN):
            waits = [("RF", 2 + k)] + ([("XF", 1)] if k == PAR else [])
            tasks.append(Task("farc", q, waits, [("ZF", k), ("ZF", 2 + k)], [("IF", k)], cost=unit * 1.3,
                              args=(k,), sends=[
                (("AF", 2 + k), ("IF", 1 - k), "partner", "S"),
                (("AF", 2 + k), ("EN", 3 - k), "outer", "R")]))
        for dz in (0, 2):
            for k in (PAR, OWN):
                waits = [("RN", dz * 3 + k)] + ([("XN", dz)] if k == PAR else [])
                tasks.append(Task("nearz", q, waits, [("EN", dz * 2 + k)], cost=unit * 1.3, args=(dz, k), sends=[
                    (("AZ", dz + k), ("ZN", (0 if dz == 0 else 2) + k), "zm" if dz == 0 else "zp", None)]))
        tasks.append(Task("nearp", q, [("RN", 3 + PAR), ("XN", 1), ("ZN", PAR), ("ZN", 2 + PAR)],
                          [("EN", 2 + PAR)], cost=unit * 1.6, sends=[
            (("AI", 0), ("IN", 0), "partner", None)]))
        tasks.append(Task("last", q, [("RN", 3 + OWN), ("ZN", OWN), ("ZN", 2 + OWN), ("IN", 0)],
                          [("EN", 2 + OWN)], cost=unit * 1.6))
    tasks.append(Task("forward", None, [("H", i) for i in range(27) if i != 3], cost=3.0))
    return tasks


BUFFERS = {
    "H": (28, True), "F": (6, True),
    "O": (18, False), "AX": (3, False), "AF": (6, False), "AZ": (4, False), "AI": (1, False),
    "RN": (9, False), "RF": (6, False), "XN": (3, False), "XF": (3, False), "ZF": (4, False),
    "IF": (2, False), "EN": (6, False), "ZN": (4, False), "IN": (1, False),
}
RECEIVED = ("H", "F", "RN", "RF", "XN", "XF", "ZF", "IF", "EN", "ZN", "IN")


def kernel(chunks, order, off_ref, cnt_ref, dens_ref, tile_hbm, out_ref, *scratch):
    names = list(BUFFERS)
    buf = dict(zip(names, scratch[:len(names)]))
    tiles, part, flip, total, back, chosen, local_sem, send_sem, recv_sem = scratch[len(names):]
    gx, gy, gz = lax.axis_index("gx"), lax.axis_index("gy"), lax.axis_index("gz")
    nx, ny, nz = lax.axis_size("gx"), lax.axis_size("gy"), lax.axis_size("gz")
    b, c = lax.rem(gx, 2), lax.rem(gy, 2)
    sender = b == c
    receiver = b != c
    xd = lax.rem(gx + 2 - 4 * b + nx, nx)
    xp = lax.rem(gx - 2 + 4 * b + nx, nx)
    sib = gy + 1 - 2 * c
    outer_x = lax.rem(gx + 1 - 2 * b + nx, nx)
    where_to = {
        "partner": (outer_x, gy, gz),
        "outer": (outer_x, lax.rem(gy - 2 + 4 * b + ny, ny), gz),
        "sib": (gx, sib, gz),
        "xd": (xd, gy, gz), "xp": (xp, gy, gz),
        "sxd": (xd, sib, gz), "sxp": (xp, sib, gz),
        "zp": (gx, gy, lax.rem(gz + 1, nz)),
        "zm": (gx, gy, lax.rem(gz + nz - 1, nz)),
    }
    rows, columns = buf["H"].shape[1:]
    slots = tiles.shape[0]

    density_copy = pltpu.make_async_copy(dens_ref.at[0, 0, 0], buf["H"].at[3], local_sem.at[slots])
    density_copy.start()
    for s in range(slots):
        pltpu.make_async_copy(tile_hbm.at[0, 0, 0, s], tiles.at[s], local_sem.at[s]).start()
    barrier = pltpu.get_barrier_semaphore()
    for target in where_to.values():
        pl.semaphore_signal(barrier, inc=1, device_id=target, device_id_type=MESH)

    live = cnt_ref[0, 0, 0]
    home = []
    for s in range(slots):
        code = off_ref[0, 0, 0, s]
        dx, dy, dz = lax.div(code, 9), lax.rem(lax.div(code, 3), 3), lax.rem(code, 3)
        k = jnp.where(dx == 1, OWN, jnp.where(dx == 2 - 2 * b, PAR, CRS))
        group = jnp.where(dy == 1, 0, jnp.where(dy == 2 - 2 * c, 1, 2))
        home.append(jnp.where(s < live, group * 9 + dz * 3 + k, 27))
        chosen[27 + s] = home[s]

    @pl.loop(0, 27)
    def _(h):
        index = jnp.int32(slots)
        for s in range(slots):
            index = jnp.where(home[s] == h, s, index)
        chosen[h] = index

    buf["H"][27] = jnp.zeros((rows, columns), jnp.bfloat16)
    part[slots] = jnp.zeros((columns, rows), jnp.bfloat16)
    density_copy.wait()
    pl.semaphore_wait(barrier, len(where_to))

    def piece(name, index, q):
        size = (rows if BUFFERS[name][1] else columns) // chunks
        return buf[name].at[index, pl.ds(q * size, size)]

    first_sem = {}
    count = 0
    for name in RECEIVED:
        first_sem[name] = count
        count += BUFFERS[name][0] * chunks

    def arrival(name, index, q):
        return recv_sem.at[first_sem[name] + index * chunks + q]

    waited = set()

    def wait_for(key, q):
        if (key, q) in waited:
            return
        waited.add((key, q))
        ref = piece(key[0], key[1], q)
        pltpu.make_async_copy(ref, ref, arrival(key[0], key[1], q)).wait()

    in_flight = []

    def send(item, q):
        source, target, to, role = item
        copy = pltpu.make_async_remote_copy(
            src_ref=piece(source[0], source[1], q),
            dst_ref=piece(target[0], target[1], q),
            send_sem=send_sem.at[len(in_flight)],
            recv_sem=arrival(target[0], target[1], q),
            device_id=where_to[to],
            device_id_type=MESH,
        )
        in_flight.append((copy, role))
        return copy

    strip = 32
    height = columns // chunks

    def add(target, q, terms, own=None):
        @pl.loop(0, height // strip)
        def _(i):
            span = pl.ds(pl.multiple_of(q * height + i * strip, strip), strip)
            value = None
            if own is not None:
                value = part[chosen[own], span].astype(jnp.float32)
            for name, index in terms:
                term = buf[name][index, span].astype(jnp.float32)
                value = term if value is None else value + term
            if target is None:
                back[span] = value
            else:
                buf[target[0]][target[1], span] = value.astype(jnp.bfloat16)

    def partials():
        flip[...] = buf["H"][3].T

        @pl.loop(0, slots)
        def _(s):
            pltpu.make_async_copy(tile_hbm.at[0, 0, 0, s], tiles.at[s], local_sem.at[s]).wait()
            part[s] = jnp.dot(flip[...], tiles[s], preferred_element_type=jnp.float32).astype(jnp.bfloat16)

    def forward():
        total[...] = jnp.zeros_like(total)

        @pl.loop(0, slots)
        def _(s):
            total[...] += jnp.dot(tiles[s], buf["H"][chosen[27 + s]], preferred_element_type=jnp.float32)

    tasks = make_tasks(chunks)
    for number in order:
        task = tasks[number]
        spans = range(chunks) if task.q is None else [task.q]
        for key in task.waits:
            for q in spans:
                wait_for(key, q)
        q = task.q
        kind, args = task.kind, task.args
        by_role = {}
        if kind == "part":
            partials()
        elif kind == "forward":
            forward()
        elif kind == "sel":
            group, dz, k = args
            buf["O"][(group - 1) * 9 + dz * 3 + k] = part[chosen[group * 9 + dz * 3 + k]]
        elif kind == "cross":
            add(("AX", args[0]), q, [("RN", args[0] * 3 + CRS)], own=args[0] * 3 + CRS)
        elif kind == "farz":
            dz = args[0]
            add(("AF", dz * 2 + PAR), q, [("RF", dz * 2 + PAR), ("XF", dz)])
        elif kind == "farc":
            k = args[0]
            terms = [("RF", 2 + k)] + ([("XF", 1)] if k == PAR else [])
            by_role["S"] = functools.partial(add, ("AF", 2 + k), q, terms + [("ZF", k), ("ZF", 2 + k)])
            by_role["R"] = functools.partial(add, ("AF", 2 + k), q, terms + [("IF", k)])
        elif kind == "nearz":
            dz, k = args
            terms = [("RN", dz * 3 + k)] + ([("XN", dz)] if k == PAR else [])
            by_role["S"] = functools.partial(add, ("AZ", dz + k), q, terms + [("EN", dz * 2 + k)], own=dz * 3 + k)
            by_role["R"] = functools.partial(add, ("AZ", dz + k), q, terms, own=dz * 3 + k)
        elif kind == "nearp":
            terms = [("RN", 3 + PAR), ("XN", 1), ("ZN", PAR), ("ZN", 2 + PAR)]
            by_role["S"] = functools.partial(add, ("AI", 0), q, terms + [("EN", 2 + PAR)], own=3 + PAR)
            by_role["R"] = functools.partial(add, ("AI", 0), q, terms, own=3 + PAR)
        elif kind == "last":
            terms = [("RN", 3 + OWN), ("ZN", OWN), ("ZN", 2 + OWN), ("IN", 0)]
            by_role["S"] = functools.partial(add, None, q, terms + [("EN", 2 + OWN)], own=3 + OWN)
            by_role["R"] = functools.partial(add, None, q, terms, own=3 + OWN)

        copies = {None: [], "S": [], "R": []}
        for item in task.sends:
            for span in spans:
                copies[item[3]].append(send(item, span))
        for role, flag, keys in (("S", sender, task.waits_s), ("R", receiver, task.waits_r)):
            if keys or copies[role] or role in by_role:
                @pl.when(flag)
                def _():
                    for key in keys:
                        for span in spans:
                            wait_for(key, span)
                    if role in by_role:
                        by_role[role]()
                    for copy in copies[role]:
                        copy.start()
        for copy in copies[None]:
            copy.start()

    out_ref[0, 0, 0] = (total[...] + back[...].T).astype(out_ref.dtype)
    for role, flag in ((None, None), ("S", sender), ("R", receiver)):
        def drain():
            for copy, which in in_flight:
                if which == role:
                    copy.wait_send()
        if role is None:
            drain()
        else:
            pl.when(flag)(drain)


def local(density, integrals, offsets, counts):
    rows, columns = density.shape[3:]
    slots = integrals.shape[3]
    tasks = make_tasks(CHUNKS)
    sends = sum(len(t.sends) * (CHUNKS if t.q is None else 1) for t in tasks)
    arrivals = sum(BUFFERS[name][0] for name in RECEIVED) * CHUNKS
    scratch = [
        pltpu.VMEM((n, rows, columns) if straight else (n, columns, rows), jnp.bfloat16)
        for n, straight in BUFFERS.values()
    ]
    scratch += [
        pltpu.VMEM((slots, rows, rows), jnp.bfloat16),
        pltpu.VMEM((slots + 1, columns, rows), jnp.bfloat16),
        pltpu.VMEM((columns, rows), jnp.bfloat16),
        pltpu.VMEM((rows, columns), jnp.float32),
        pltpu.VMEM((columns, rows), jnp.float32),
        pltpu.SMEM((27 + slots,), jnp.int32),
        pltpu.SemaphoreType.DMA((slots + 1,)),
        pltpu.SemaphoreType.DMA((sends,)),
        pltpu.SemaphoreType.DMA((arrivals,)),
    ]
    return pl.pallas_call(
        functools.partial(kernel, CHUNKS, ORDER),
        out_shape=jax.ShapeDtypeStruct(density.shape, density.dtype),
        in_specs=[
            pl.BlockSpec(memory_space=pltpu.SMEM),
            pl.BlockSpec(memory_space=pltpu.SMEM),
            pl.BlockSpec(memory_space=pl.ANY),
            pl.BlockSpec(memory_space=pl.ANY),
        ],
        out_specs=pl.BlockSpec(memory_space=pltpu.VMEM),
        scratch_shapes=scratch,
        compiler_params=pltpu.CompilerParams(
            collective_id=0, has_side_effects=True, vmem_limit_bytes=56 * 1024 * 1024
        ),
    )(offsets, counts, density, integrals)


def solution(mesh):
    return jax.shard_map(
        local,
        mesh=mesh,
        in_specs=(
            P("gx", "gy", "gz", None, None),
            P("gx", "gy", "gz", None, None, None),
            P("gx", "gy", "gz", None),
            P("gx", "gy", "gz"),
        ),
        out_specs=P("gx", "gy", "gz", None, None),
        check_vma=False,
    )
```

time: 160 us -> 73.6 us (0.46)
  the two profiles are of different devices: /device:TPU:1 before, /device:TPU:28 now
where the time goes in v1:
time: 73.6 us; the launch traced here: 73.5 us
  Pallas kernels  71.1 us (97%)
  local copies, waits for them, and re-layouts  1.67 us (2%)
    pallas_call x1, Pallas kernels, local(): pl.pallas_call(functools.partial(kernel, CHUNKS, ORDER), out_shape=jax.Sh...  71.1 us
    unnamed x1, local copies, waits for them, and re-layouts  1.67 us

profile of v1, /device:TPU:28, one launch (start us, length us, event | category | flops | bytes accessed | tf_op | source)
XLA Modules:
  0.0 73.5 jit_solution(13901616006835326098)
XLA Ops:
  0.7 71.1 %shard_map.46 = bf16[1,1,1,512,256]{4,3,2,1,0:T(8,128)(2,1)} custom-call(s32[1,1,1,9]{3,2,1,0:T(1,128)} %off_ref.1, s32[1,1,1]{2,1,0:T(1,128)S(6)} %copy.6.cnt_ref, bf16[1,1,1,512,256]{4,3,2,1,0:T(8,128)(2,1)} %dens_ref.1, bf16[1,1,1,9,512,512]{5,4,3,2,1,0:T(8,128)(2,1)} %tile_hbm.1), custom_call_target="tpu_custom_call" | custom-call | tf_op jit(solution)/shard_map/pallas_call | solution.py:366
  71.8 1.7 %copy.7 = bf16[1,1,1,512,256]{4,3,2,1,0:T(8,128)(2,1)} copy(bf16[1,1,1,512,256]{4,3,2,1,0:T(8,128)(2,1)} %shard_map.46) | data formatting | bytes 524288

commit v2 on v0

v2 whole, which is shorter than its diff:
```python
import functools

import jax
import jax.numpy as jnp
from jax import lax
from jax.experimental import pallas as pl
from jax.experimental.pallas import tpu as pltpu
from jax.sharding import PartitionSpec as P

MESH = pl.DeviceIdType.MESH
OWN, PAR, CRS = 0, 1, 2
VMEM_LIMIT = 56164352
D_SIZES = (4, 4, 8)
P_SIZES = (8, 8)
X_FIRST = ()
ORDER = {
    "S": (
        0, 1, 2, 45, 46, 47, 48, 49, 50, 51, 52, 53, 3, 4, 6, 54, 55, 56, 57, 58, 59, 60, 61, 62, 63, 69,
        17, 18, 20, 90, 73, 94, 8, 77, 98, 64, 85, 31, 32, 34, 65, 67, 86, 22, 5, 7, 11, 19, 21, 25, 88, 36,
        33, 39, 71, 9, 14, 10, 80, 28, 66, 92, 23, 24, 101, 42, 35, 87, 75, 12, 13, 37, 82, 26, 27, 96, 106,
        103, 40, 41, 15, 16, 107, 29, 38, 79, 43, 30, 100, 84, 81, 105, 44, 102, 83, 104, 108,
    ),
    "R": (
        0, 1, 2, 45, 14, 46, 47, 48, 49, 50, 51, 52, 3, 4, 6, 28, 53, 54, 55, 56, 57, 58, 59, 60, 61, 62,
        63, 17, 18, 20, 42, 11, 15, 64, 8, 85, 16, 31, 32, 34, 65, 86, 79, 100, 25, 29, 81, 5, 7, 102, 22,
        30, 80, 101, 82, 68, 19, 21, 103, 39, 43, 89, 33, 44, 72, 66, 12, 36, 13, 93, 35, 87, 26, 9, 76, 27,
        10, 97, 70, 40, 23, 91, 83, 24, 74, 41, 104, 95, 78, 37, 106, 99, 38, 107, 108, 84, 105,
    ),
}


def slot(group, dz, k):
    return ("H", group * 9 + dz * 3 + k)


def far(dz, k):
    return ("F", dz * 2 + k)


def out_slot(group, dz, k):
    return ("O", (group - 1) * 9 + dz * 3 + k)


class Task:
    def __init__(self, kind, q, waits=(), waits_s=(), waits_r=(), sends=(), cost=0.0, args=(), role=None):
        self.kind = kind
        self.q = q
        self.waits = list(waits)
        self.waits_s = list(waits_s)
        self.waits_r = list(waits_r)
        self.sends = list(sends)
        self.cost = cost
        self.args = args
        self.role = role


def make_tasks(d_sizes, p_sizes, x_first=()):
    tasks = []
    for q in range(len(d_sizes)):
        c = slot(0, 1, OWN)
        tasks.append(Task("relay", q, sends=[
            (c, slot(0, 1, PAR), "partner", None),
            (c, slot(0, 0, OWN), "zp", None),
            (c, slot(0, 2, OWN), "zm", None),
            (c, far(1, PAR), "outer", "S"),
            (c, slot(1, 1, OWN), "sib", None),
        ]))
    for q in range(len(d_sizes)):
        c = slot(0, 1, PAR)
        tasks.append(Task("relay", q, [c], sends=[
            (c, slot(0, 1, CRS), "xd", None),
            (c, far(1, OWN), "outer", "S"),
            (c, slot(0, 0, PAR), "zp", None),
            (c, slot(0, 2, PAR), "zm", None),
            (c, slot(1, 1, PAR), "sib", None),
        ]))
        for dz in (0, 2):
            c = slot(0, dz, OWN)
            tasks.append(Task("relay", q, [c], sends=[
                (c, far(dz, PAR), "outer", "S"),
                (c, slot(1, dz, OWN), "sib", None),
            ]))
            c = slot(0, dz, PAR)
            sends = [(c, far(dz, OWN), "outer", "S")]
            if q not in x_first:
                sends.append((c, slot(0, dz, CRS), "xd", None))
            sends.append((c, slot(1, dz, PAR), "sib", None))
            tasks.append(Task("relay", q, [c], sends=sends))
        for dz in (1, 0, 2):
            c = slot(0, dz, CRS)
            sends = [(c, slot(1, dz, CRS), "sib", None)]
            if dz == 1 and q in x_first:
                sends = [(c, slot(0, 0, CRS), "zp", None), (c, slot(0, 2, CRS), "zm", None)] + sends
            tasks.append(Task("relay", q, [c], sends=sends))
        for k in (OWN, PAR):
            for dz in (1, 0, 2):
                c = far(dz, k)
                sends = []
                if dz == 1:
                    sends += [
                        (c, far(1, 1 - k), "partner", "R"),
                        (c, far(0, k), "zp", "S"),
                        (c, far(2, k), "zm", "S"),
                    ]
                if k == PAR:
                    sends.append((c, slot(2, dz, CRS), "sxd", None))
                sends.append((c, slot(2, dz, k), "sib", None))
                tasks.append(Task("relay", q, [c], sends=sends))
    tasks.append(Task("part", None, cost=2.9))
    for dz in (0, 2, 1):
        for k in (CRS, PAR, OWN):
            send = (out_slot(2, dz, k), ("RF", dz * 2 + k), "sib", None)
            if k == CRS:
                send = (out_slot(2, dz, k), ("XF", dz), "sxp", None)
            tasks.append(Task("sel", None, cost=0.03, args=(2, dz, k), sends=[send]))
    for k in (CRS, PAR, OWN):
        for dz in (0, 2, 1):
            tasks.append(Task("sel", None, cost=0.03, args=(1, dz, k), sends=[
                (out_slot(1, dz, k), ("RN", dz * 3 + k), "sib", None)]))
    for q, size in enumerate(p_sizes):
        unit = 0.14 * size / 16
        for dz in (0, 2):
            tasks.append(Task("add", q, [("RN", dz * 3 + CRS)], cost=unit, args=(("AX", dz), dz * 3 + CRS), sends=[
                (("AX", dz), ("ZX", dz // 2), "zm" if dz == 0 else "zp", None)]))
        tasks.append(Task("add", q, [("RN", 3 + CRS), ("ZX", 0), ("ZX", 1)], cost=unit * 1.5,
                          args=(("AX", 1), 3 + CRS), sends=[(("AX", 1), ("XN", 0), "xp", None)]))
        for dz in (0, 2, 1):
            for k in (PAR, OWN):
                here = ("AF", dz * 2 + k)
                waits = [("RF", dz * 2 + k)] + ([("XF", dz)] if k == PAR else [])
                if k == PAR:
                    tasks.append(Task("add", q, waits_s=waits, role="S", cost=unit, args=(here, None), sends=[
                        (here, ("IF", dz * 2 + 1 - k), "partner", "S")]))
                else:
                    tasks.append(Task("relay", q, waits_s=waits, role="S", sends=[
                        (waits[0], ("IF", dz * 2 + 1 - k), "partner", "S")]))
                tasks.append(Task("add", q, waits_r=waits + [("IF", dz * 2 + k)], role="R", cost=unit * 1.2,
                                  args=(here, None), sends=[(here, ("EN", dz * 2 + 1 - k), "outer", "R")]))
        for dz in (0, 2):
            for k in (PAR, OWN):
                tasks.append(Task("add", q, [("RN", dz * 3 + k)], [("EN", dz * 2 + k)], cost=unit * 1.2,
                                  args=(("AZ", dz + k), dz * 3 + k), sends=[
                    (("AZ", dz + k), ("ZN", dz + k), "zm" if dz == 0 else "zp", None)]))
        tasks.append(Task("add", q, [("RN", 3 + PAR), ("XN", 0), ("ZN", PAR), ("ZN", 2 + PAR)],
                          [("EN", 2 + PAR)], cost=unit * 1.6, args=(("AI", 0), 3 + PAR), sends=[
            (("AI", 0), ("IN", 0), "partner", None)]))
        tasks.append(Task("add", q, [("RN", 3 + OWN), ("ZN", OWN), ("ZN", 2 + OWN), ("IN", 0)],
                          [("EN", 2 + OWN)], cost=unit * 1.6, args=(None, 3 + OWN)))
    for q, size in enumerate(d_sizes):
        tasks.append(Task("forward", q, [("H", i) for i in range(27) if i != 3], cost=0.2 + 2.7 * size / 16))
    return tasks


BUFFERS = {
    "H": (28, True), "F": (6, True),
    "O": (18, False), "AX": (3, False), "AF": (6, False), "AZ": (4, False), "AI": (1, False),
    "RN": (9, False), "RF": (6, False), "XN": (1, False), "XF": (3, False), "ZX": (2, False),
    "IF": (6, False), "EN": (6, False), "ZN": (4, False), "IN": (1, False),
}
RECEIVED = ("H", "F", "RN", "RF", "XN", "XF", "ZX", "IF", "EN", "ZN", "IN")


def chunks_of(name):
    sizes = D_SIZES if BUFFERS[name][1] else P_SIZES
    return [(sum(sizes[:i]), size) for i, size in enumerate(sizes)]


def places(name, rows, columns):
    unit = (rows if BUFFERS[name][1] else columns) // 16
    return [(first * unit, size * unit) for first, size in chunks_of(name)]


def kernel(off_hbm, cnt_hbm, dens_ref, tile_hbm, out_ref, *scratch):
    names = list(BUFFERS)
    halo = scratch[:len(D_SIZES)]
    scratch = scratch[len(D_SIZES):]
    buf = dict(zip(names[1:], scratch[:len(names) - 1]))
    tiles = scratch[len(names) - 1:len(names) - 1 + len(D_SIZES)]
    (square, part, flip, picked, total, back, off_ref, cnt_ref, chosen,
     local_sem, tile_sem, send_sem, recv_sem) = scratch[len(names) - 1 + len(D_SIZES):]
    gx, gy, gz = lax.axis_index("gx"), lax.axis_index("gy"), lax.axis_index("gz")
    nx, ny, nz = lax.axis_size("gx"), lax.axis_size("gy"), lax.axis_size("gz")
    b, c = lax.rem(gx, 2), lax.rem(gy, 2)
    xd = lax.rem(gx + 2 - 4 * b + nx, nx)
    xp = lax.rem(gx - 2 + 4 * b + nx, nx)
    sib = gy + 1 - 2 * c
    outer_x = lax.rem(gx + 1 - 2 * b + nx, nx)
    where_to = {
        "partner": (outer_x, gy, gz),
        "outer": (outer_x, lax.rem(gy - 2 + 4 * b + ny, ny), gz),
        "sib": (gx, sib, gz),
        "xd": (xd, gy, gz), "xp": (xp, gy, gz),
        "sxd": (xd, sib, gz), "sxp": (xp, sib, gz),
        "zp": (gx, gy, lax.rem(gz + 1, nz)),
        "zm": (gx, gy, lax.rem(gz + nz - 1, nz)),
    }
    rows, columns = total.shape
    slots = off_ref.shape[-1]
    d_places = places("H", rows, columns)

    barrier = pltpu.get_barrier_semaphore()
    for target in where_to.values():
        pl.semaphore_signal(barrier, inc=1, device_id=target, device_id_type=MESH)
    density_copies = []
    for q, (first, size) in enumerate(d_places):
        copy = pltpu.make_async_copy(
            dens_ref.at[0, 0, 0, pl.ds(first, size)], halo[q].at[3], local_sem.at[slots + q])
        copy.start()
        density_copies.append(copy)
    index_copies = [
        pltpu.make_async_copy(off_hbm, off_ref, local_sem.at[slots + len(d_places)]),
        pltpu.make_async_copy(cnt_hbm, cnt_ref, local_sem.at[slots + len(d_places) + 1]),
    ]
    for copy in index_copies:
        copy.start()

    def tile_copy(s, q):
        first, size = d_places[q]
        return pltpu.make_async_copy(
            tile_hbm.at[0, 0, 0, s, :, pl.ds(first, size)], tiles[q].at[:, pl.ds(s * size, size)],
            tile_sem.at[s * len(d_places) + q])

    for s in range(slots):
        pltpu.make_async_copy(tile_hbm.at[0, 0, 0, s], square.at[s], local_sem.at[s]).start()

    def piece(name, index, q):
        if name == "H":
            return halo[q].at[index]
        first, size = places(name, rows, columns)[q]
        return buf[name].at[index, pl.ds(first, size)]

    first_sem = {}
    count = 0
    for name in RECEIVED:
        first_sem[name] = count
        count += BUFFERS[name][0] * len(chunks_of(name))

    def arrival(name, index, q):
        return recv_sem.at[first_sem[name] + index * len(chunks_of(name)) + q]

    def add(target, q, terms, own):
        first, size = places("AF", rows, columns)[q]
        strip = 32

        @pl.loop(0, size // strip)
        def _(i):
            span = pl.ds(pl.multiple_of(first + i * strip, strip), strip)
            value = None
            if own is not None:
                value = part[chosen[own], span].astype(jnp.float32)
            for name, index in terms:
                term = buf[name][index, span].astype(jnp.float32)
                value = term if value is None else value + term
            if target is None:
                back[span] = value
            else:
                buf[target[0]][target[1], span] = value.astype(jnp.bfloat16)

    def find_tiles():
        live = cnt_ref[0, 0, 0]
        home = []
        for s in range(slots):
            code = off_ref[0, 0, 0, s]
            dx, dy, dz = lax.div(code, 9), lax.rem(lax.div(code, 3), 3), lax.rem(code, 3)
            k = jnp.where(dx == 1, OWN, jnp.where(dx == 2 - 2 * b, PAR, CRS))
            group = jnp.where(dy == 1, 0, jnp.where(dy == 2 - 2 * c, 1, 2))
            home.append(jnp.where(s < live, group * 9 + dz * 3 + k, 27))
            chosen[27 + s] = home[s]

        @pl.loop(0, 27)
        def _(h):
            index = jnp.int32(slots)
            for s in range(slots):
                index = jnp.where(home[s] == h, s, index)
            chosen[h] = index

    def partials():
        for q, (first, size) in enumerate(d_places):
            flip[:, first:first + size] = halo[q][3].T
            halo[q][27] = jnp.zeros((size, columns), jnp.bfloat16)
        part[slots] = jnp.zeros((columns, rows), jnp.bfloat16)
        total[...] = jnp.zeros_like(total)
        for copy in index_copies:
            copy.wait()
        find_tiles()

        @pl.loop(0, slots)
        def _(s):
            pltpu.make_async_copy(tile_hbm.at[0, 0, 0, s], square.at[s], local_sem.at[s]).wait()
            part[s] = jnp.dot(flip[...], square[s], preferred_element_type=jnp.float32).astype(jnp.bfloat16)

        for s in range(slots):
            for q in range(len(d_places)):
                tile_copy(s, q).start()

    def forward(q):
        size = d_places[q][1]
        for s in range(slots):
            tile_copy(s, q).wait()
            picked[s * size:(s + 1) * size] = halo[q][chosen[27 + s]]
        total[...] += jnp.dot(tiles[q][...], picked[:slots * size], preferred_element_type=jnp.float32)

    tasks = make_tasks(D_SIZES, P_SIZES, X_FIRST)

    def run(role):
        waited = set()
        in_flight = []
        for number in ORDER[role]:
            task = tasks[number]
            keys = task.waits + (task.waits_s if role == "S" else task.waits_r)
            for name, index in keys:
                if (name, index, task.q) not in waited:
                    waited.add((name, index, task.q))
                    ref = piece(name, index, task.q)
                    pltpu.make_async_copy(ref, ref, arrival(name, index, task.q)).wait()
            if task.kind == "part":
                partials()
            elif task.kind == "forward":
                forward(task.q)
            elif task.kind == "sel":
                group, dz, k = task.args
                buf["O"][(group - 1) * 9 + dz * 3 + k] = part[chosen[group * 9 + dz * 3 + k]]
            elif task.kind == "add":
                add(task.args[0], task.q, keys, task.args[1])
            elif number < len(D_SIZES):
                density_copies[number].wait()
            for source, target, to, only in task.sends:
                if only in (None, role):
                    for q in range(len(P_SIZES)) if task.q is None else [task.q]:
                        copy = pltpu.make_async_remote_copy(
                            src_ref=piece(source[0], source[1], q),
                            dst_ref=piece(target[0], target[1], q),
                            send_sem=send_sem.at[len(in_flight)],
                            recv_sem=arrival(target[0], target[1], q),
                            device_id=where_to[to],
                            device_id_type=MESH,
                        )
                        copy.start()
                        in_flight.append(copy)
        out_ref[0, 0, 0] = (total[...] + back[...].T).astype(out_ref.dtype)
        for copy in in_flight:
            copy.wait_send()

    pl.semaphore_wait(barrier, len(where_to))
    pl.when(b == c)(functools.partial(run, "S"))
    pl.when(b != c)(functools.partial(run, "R"))


def local(density, integrals, offsets, counts):
    rows, columns = density.shape[3:]
    slots = integrals.shape[3]
    tasks = make_tasks(D_SIZES, P_SIZES, X_FIRST)
    sends = sum(len(t.sends) * (len(P_SIZES) if t.q is None else 1) for t in tasks)
    arrivals = sum(BUFFERS[name][0] * len(chunks_of(name)) for name in RECEIVED)
    scratch = [pltpu.VMEM((BUFFERS["H"][0], size, columns), jnp.bfloat16) for _, size in places("H", rows, columns)]
    scratch += [
        pltpu.VMEM((n, rows, columns) if straight else (n, columns, rows), jnp.bfloat16)
        for name, (n, straight) in BUFFERS.items() if name != "H"
    ]
    scratch += [
        pltpu.VMEM((rows, slots * size), jnp.bfloat16) for _, size in places("H", rows, columns)
    ]
    scratch += [
        pltpu.VMEM((slots, rows, rows), jnp.bfloat16),
        pltpu.VMEM((slots + 1, columns, rows), jnp.bfloat16),
        pltpu.VMEM((columns, rows), jnp.bfloat16),
        pltpu.VMEM((slots * max(size for _, size in places("H", rows, columns)), columns), jnp.bfloat16),
        pltpu.VMEM((rows, columns), jnp.float32),
        pltpu.VMEM((columns, rows), jnp.float32),
        pltpu.SMEM(offsets.shape, jnp.int32),
        pltpu.SMEM(counts.shape, jnp.int32),
        pltpu.SMEM((27 + slots,), jnp.int32),
        pltpu.SemaphoreType.DMA((slots + len(D_SIZES) + 2,)),
        pltpu.SemaphoreType.DMA((slots * len(D_SIZES),)),
        pltpu.SemaphoreType.DMA((sends,)),
        pltpu.SemaphoreType.DMA((arrivals,)),
    ]
    return pl.pallas_call(
        kernel,
        out_shape=jax.ShapeDtypeStruct(density.shape, density.dtype),
        in_specs=[
            pl.BlockSpec(memory_space=pl.ANY),
            pl.BlockSpec(memory_space=pl.ANY),
            pl.BlockSpec(memory_space=pl.ANY),
            pl.BlockSpec(memory_space=pl.ANY),
        ],
        out_specs=pl.BlockSpec(memory_space=pltpu.VMEM),
        scratch_shapes=scratch,
        compiler_params=pltpu.CompilerParams(
            collective_id=0, has_side_effects=True, vmem_limit_bytes=VMEM_LIMIT
        ),
    )(offsets, counts, density, integrals)


def solution(mesh):
    return jax.shard_map(
        local,
        mesh=mesh,
        in_specs=(
            P("gx", "gy", "gz", None, None),
            P("gx", "gy", "gz", None, None, None),
            P("gx", "gy", "gz", None),
            P("gx", "gy", "gz"),
        ),
        out_specs=P("gx", "gy", "gz", None, None),
        check_vma=False,
    )
```

time: 160 us -> 63.2 us (0.40)
  waiting for transfers between devices: 61.5 us -> 0 us
  Pallas kernels: 0 us -> 61.1 us
  starting transfers between devices: 49.1 us -> 0 us
  local copies, waits for them, and re-layouts: 24.2 us -> 1.35 us
  matrix products: 18.9 us -> 0 us
  other arithmetic: 4.19 us -> 0 us
    ppermute x12 -> x0, waiting for transfers between devices: 61.5 us -> none  [the longest x6 34.2 us: extended_2(): lax.ppermute(lax.slice_in_dim(block, block.shape[dim] - width, None, axis...]
    pallas_call x0 -> x1, Pallas kernels: none -> 61.1 us  [local(): pl.pallas_call(kernel, out_shape=jax.ShapeDtypeStruct(density.shape, dens...]
    ppermute x12 -> x0, starting transfers between devices: 49.1 us -> none  [the longest x6 26.8 us: extended_2(): lax.ppermute(lax.slice_in_dim(block, 0, width, axis=dim), axis, backward)]
    dot_general x4 -> x0, matrix products: 18.9 us -> none  [the longest x1 5.99 us: local(): jnp.einsum('so,obc->sbc', selector, neighbours, preferred_element_type=jn...]
    convert_element_type x1 -> x0, local copies, waits for them, and re-layouts: 13.6 us -> none  [local(): outgoing = jnp.einsum('so,sic->oic', selector, partial_value, preferred_e...]
    dot_general x1 -> x0, local copies, waits for them, and re-layouts: 5.91 us -> none  [local(): jnp.einsum('so,obc->sbc', selector, neighbours, preferred_element_type=jn...]
    slice x3 -> x0, local copies, waits for them, and re-layouts: 3.75 us -> none  [extended_2(): lax.slice_in_dim(block, block.shape[dim] - width, None, axis=dim)]
    convert_element_type x2 -> x0, other arithmetic: 3.08 us -> none  [the longest x1 2.67 us: collect_ydir(): buffer.astype(jnp.bfloat16)]
  transfers between devices with their start and end apart: 12 -> 0, of which waited for: 8 -> 0; matrix products, arithmetic and copies ran while one was open for 11% -> 0% of each run, Pallas kernels for 0% -> 0%
where the time goes in v2:
time: 63.2 us; the launch traced here: 63.1 us
  Pallas kernels  61.1 us (97%)
  local copies, waits for them, and re-layouts  1.35 us (2%)
  between operations  0.67 us (1%)
    pallas_call x1, Pallas kernels, local(): pl.pallas_call(kernel, out_shape=jax.ShapeDtypeStruct(density.shape, dens...  61.1 us
    unnamed x3, local copies, waits for them, and re-layouts  1.35 us

profile of v2, /device:TPU:1, one launch (start us, length us, event | category | flops | bytes accessed | tf_op | source)
XLA Modules:
  0.0 63.1 jit_solution(36169696952204558)
XLA Ops:
  0.7 0.0 copy-start
  0.7 0.6 %copy-done = s32[1,1,1,9]{3,2,1,0:T(1,128)S(1)} copy-done((s32[1,1,1,9]{3,2,1,0:T(1,128)S(1)}, s32[1,1,1,9]{3,2,1,0:T(1,128)}, u32[]{:S(2)}) %copy-start) | copy-done | bytes 60
  1.3 61.1 %shard_map.46 = bf16[1,1,1,512,256]{4,3,2,1,0:T(8,128)(2,1)S(1)} custom-call(s32[1,1,1,9]{3,2,1,0:T(1,128)S(1)} %copy-done, s32[1,1,1]{2,1,0:T(1,128)S(6)} %copy.6.cnt_hbm, bf16[1,1,1,512,256]{4,3,2,1,0:T(8,128)(2,1)} %dens_ref.1, bf16[1,1,1,9,512,512]{5,4,3,2,1,0:T(8,128)(2,1)} %tile_hbm.1), custom_call_target="tpu_custom_call" | custom-call | tf_op jit(solution)/shard_map/pallas_call | solution.py:378
  62.4 0.7 %copy.7 = bf16[1,1,1,512,256]{4,3,2,1,0:T(8,128)(2,1)} copy(bf16[1,1,1,512,256]{4,3,2,1,0:T(8,128)(2,1)S(1)} %shard_map.46) | data formatting | bytes 524288
Async XLA Ops:
  0.7 0.7 %copy-start = (s32[1,1,1,9]{3,2,1,0:T(1,128)S(1)}, s32[1,1,1,9]{3,2,1,0:T(1,128)}, u32[]{:S(2)}) copy-start(s32[1,1,1,9]{3,2,1,0:T(1,128)} %off_hbm.1) | copy-start | bytes 112

commit v3 on v2

--- a/solution.py
+++ b/solution.py
@@ -106,7 +106,7 @@
                     sends.append((c, slot(2, dz, CRS), "sxd", None))
                 sends.append((c, slot(2, dz, k), "sib", None))
                 tasks.append(Task("relay", q, [c], sends=sends))
-    tasks.append(Task("part", None, cost=2.9))
+    tasks.append(Task("part", None, cost=3.2))
     for dz in (0, 2, 1):
         for k in (CRS, PAR, OWN):
             send = (out_slot(2, dz, k), ("RF", dz * 2 + k), "sib", None)
@@ -147,9 +147,11 @@
         tasks.append(Task("add", q, [("RN", 3 + OWN), ("ZN", OWN), ("ZN", 2 + OWN), ("IN", 0)],
                           [("EN", 2 + OWN)], cost=unit * 1.6, args=(None, 3 + OWN)))
     for q, size in enumerate(d_sizes):
-        tasks.append(Task("forward", q, [("H", i) for i in range(27) if i != 3], cost=0.2 + 2.7 * size / 16))
+        tasks.append(Task("forward", q, [("H", i) for i in range(27) if i != 3], cost=0.1 + 2.7 * size / 16))
     return tasks
 
+
+TOGETHER, SEND_GROUPS = 18, 4
 
 BUFFERS = {
     "H": (28, True), "F": (6, True),
@@ -157,7 +159,35 @@
     "RN": (9, False), "RF": (6, False), "XN": (1, False), "XF": (3, False), "ZX": (2, False),
     "IF": (6, False), "EN": (6, False), "ZN": (4, False), "IN": (1, False),
 }
-RECEIVED = ("H", "F", "RN", "RF", "XN", "XF", "ZX", "IF", "EN", "ZN", "IN")
+
+
+def group_of(name, index):
+    if name == "H":
+        return ("near", index) if index < 9 else ("sibling",)
+    if name in ("F", "IF"):
+        return (name, index)
+    if name in ("RF", "XF"):
+        return ("far", index if name == "RF" else index * 2 + PAR)
+    if name == "ZX":
+        return ("cross", 1)
+    if name in ("XN", "IN"):
+        return ("centre", PAR if name == "XN" else OWN)
+    if name == "ZN":
+        return ("centre", index % 2)
+    dz, k = divmod(index, 3 if name == "RN" else 2)
+    if k == CRS:
+        return ("cross", dz)
+    return ("centre", k) if dz == 1 else ("outside", dz, k)
+
+
+def arrivals_of():
+    numbers = {}
+    for name in ("H", "F", "RN", "RF", "IF"):
+        for index in range(BUFFERS[name][0]):
+            for q in range(len(chunks_of(name))):
+                if name != "H" or index not in (3, 27):
+                    numbers.setdefault((group_of(name, index), q), len(numbers))
+    return numbers
 
 
 def chunks_of(name):
@@ -218,7 +248,7 @@
         first, size = d_places[q]
         return pltpu.make_async_copy(
             tile_hbm.at[0, 0, 0, s, :, pl.ds(first, size)], tiles[q].at[:, pl.ds(s * size, size)],
-            tile_sem.at[s * len(d_places) + q])
+            tile_sem.at[q])
 
     for s in range(slots):
         pltpu.make_async_copy(tile_hbm.at[0, 0, 0, s], square.at[s], local_sem.at[s]).start()
@@ -229,14 +259,18 @@
         first, size = places(name, rows, columns)[q]
         return buf[name].at[index, pl.ds(first, size)]
 
-    first_sem = {}
-    count = 0
-    for name in RECEIVED:
-        first_sem[name] = count
-        count += BUFFERS[name][0] * len(chunks_of(name))
+    numbers = arrivals_of()
 
     def arrival(name, index, q):
-        return recv_sem.at[first_sem[name] + index * len(chunks_of(name)) + q]
+        return recv_sem.at[numbers[group_of(name, index), q]]
+
+    def wait_blocks(name, n, q, semaphore):
+        if BUFFERS[name][1]:
+            ref = halo[q].at[pl.ds(0, n)]
+        else:
+            first, size = places(name, rows, columns)[q]
+            ref = buf["O"].at[pl.ds(0, n), pl.ds(first, size)]
+        pltpu.make_async_copy(ref, ref, semaphore).wait()
 
     def add(target, q, terms, own):
         first, size = places("AF", rows, columns)[q]
@@ -295,24 +329,29 @@
 
     def forward(q):
         size = d_places[q][1]
+        pltpu.make_async_copy(tiles[q], tiles[q], tile_sem.at[q]).wait()
         for s in range(slots):
-            tile_copy(s, q).wait()
             picked[s * size:(s + 1) * size] = halo[q][chosen[27 + s]]
         total[...] += jnp.dot(tiles[q][...], picked[:slots * size], preferred_element_type=jnp.float32)
 
     tasks = make_tasks(D_SIZES, P_SIZES, X_FIRST)
 
+    def send_number(straight, q, n):
+        return (q if straight else len(D_SIZES) + q) * SEND_GROUPS + n // TOGETHER
+
     def run(role):
         waited = set()
-        in_flight = []
+        sent = {}
         for number in ORDER[role]:
             task = tasks[number]
             keys = task.waits + (task.waits_s if role == "S" else task.waits_r)
-            for name, index in keys:
-                if (name, index, task.q) not in waited:
-                    waited.add((name, index, task.q))
-                    ref = piece(name, index, task.q)
-                    pltpu.make_async_copy(ref, ref, arrival(name, index, task.q)).wait()
+            groups = {}
+            for key in keys:
+                if (key, task.q) not in waited:
+                    waited.add((key, task.q))
+                    groups.setdefault(group_of(*key), []).append(key)
+            for members in groups.values():
+                wait_blocks(members[0][0], len(members), task.q, arrival(*members[0], task.q))
             if task.kind == "part":
                 partials()
             elif task.kind == "forward":
@@ -327,19 +366,22 @@
             for source, target, to, only in task.sends:
                 if only in (None, role):
                     for q in range(len(P_SIZES)) if task.q is None else [task.q]:
-                        copy = pltpu.make_async_remote_copy(
+                        straight = BUFFERS[target[0]][1]
+                        kind = (straight, q)
+                        sent[kind] = sent.get(kind, 0) + 1
+                        pltpu.make_async_remote_copy(
                             src_ref=piece(source[0], source[1], q),
                             dst_ref=piece(target[0], target[1], q),
-                            send_sem=send_sem.at[len(in_flight)],
+                            send_sem=send_sem.at[send_number(*kind, sent[kind] - 1)],
                             recv_sem=arrival(target[0], target[1], q),
                             device_id=where_to[to],
                             device_id_type=MESH,
-                        )
-                        copy.start()
-                        in_flight.append(copy)
+                        ).start()
         out_ref[0, 0, 0] = (total[...] + back[...].T).astype(out_ref.dtype)
-        for copy in in_flight:
-            copy.wait_send()
+        for (straight, q), n in sent.items():
+            for first in range(0, n, TOGETHER):
+                wait_blocks("H" if straight else "O", min(TOGETHER, n - first), q,
+                            send_sem.at[send_number(straight, q, first)])
 
     pl.semaphore_wait(barrier, len(where_to))
     pl.when(b == c)(functools.partial(run, "S"))
@@ -349,9 +391,8 @@
 def local(density, integrals, offsets, counts):
     rows, columns = density.shape[3:]
     slots = integrals.shape[3]
-    tasks = make_tasks(D_SIZES, P_SIZES, X_FIRST)
-    sends = sum(len(t.sends) * (len(P_SIZES) if t.q is None else 1) for t in tasks)
-    arrivals = sum(BUFFERS[name][0] * len(chunks_of(name)) for name in RECEIVED)
+    sends = (len(D_SIZES) + len(P_SIZES)) * SEND_GROUPS
+    arrivals = len(arrivals_of())
     scratch = [pltpu.VMEM((BUFFERS["H"][0], size, columns), jnp.bfloat16) for _, size in places("H", rows, columns)]
     scratch += [
         pltpu.VMEM((n, rows, columns) if straight else (n, columns, rows), jnp.bfloat16)
@@ -371,7 +412,7 @@
         pltpu.SMEM(counts.shape, jnp.int32),
         pltpu.SMEM((27 + slots,), jnp.int32),
         pltpu.SemaphoreType.DMA((slots + len(D_SIZES) + 2,)),
-        pltpu.SemaphoreType.DMA((slots * len(D_SIZES),)),
+        pltpu.SemaphoreType.DMA((len(D_SIZES),)),
         pltpu.SemaphoreType.DMA((sends,)),
         pltpu.SemaphoreType.DMA((arrivals,)),
     ]

time: 63.2 us -> 60.5 us (0.957)
  Pallas kernels: 61.1 us -> 58.3 us
    pallas_call x1, Pallas kernels: 61.1 us -> 58.3 us  [local(): pl.pallas_call(kernel, out_shape=jax.ShapeDtypeStruct(density.shape, dens...]
where the time goes in v3:
time: 60.5 us; the launch traced here: 60.3 us
  Pallas kernels  58.3 us (96%)
  local copies, waits for them, and re-layouts  1.35 us (2%)
  between operations  0.67 us (1%)
    pallas_call x1, Pallas kernels, local(): pl.pallas_call(kernel, out_shape=jax.ShapeDtypeStruct(density.shape, dens...  58.3 us
    unnamed x3, local copies, waits for them, and re-layouts  1.35 us

profile of v3, /device:TPU:1, one launch (start us, length us, event | category | flops | bytes accessed | tf_op | source)
XLA Modules:
  0.0 60.3 jit_solution(9065282818062108865)
XLA Ops:
  0.7 0.0 copy-start
  0.7 0.6 %copy-done = s32[1,1,1,9]{3,2,1,0:T(1,128)S(1)} copy-done((s32[1,1,1,9]{3,2,1,0:T(1,128)S(1)}, s32[1,1,1,9]{3,2,1,0:T(1,128)}, u32[]{:S(2)}) %copy-start) | copy-done | bytes 60
  1.3 58.3 %shard_map.46 = bf16[1,1,1,512,256]{4,3,2,1,0:T(8,128)(2,1)S(1)} custom-call(s32[1,1,1,9]{3,2,1,0:T(1,128)S(1)} %copy-done, s32[1,1,1]{2,1,0:T(1,128)S(6)} %copy.6.cnt_hbm, bf16[1,1,1,512,256]{4,3,2,1,0:T(8,128)(2,1)} %dens_ref.1, bf16[1,1,1,9,512,512]{5,4,3,2,1,0:T(8,128)(2,1)} %tile_hbm.1), custom_call_target="tpu_custom_call" | custom-call | tf_op jit(solution)/shard_map/pallas_call | solution.py:419
  59.6 0.7 %copy.7 = bf16[1,1,1,512,256]{4,3,2,1,0:T(8,128)(2,1)} copy(bf16[1,1,1,512,256]{4,3,2,1,0:T(8,128)(2,1)S(1)} %shard_map.46) | data formatting | bytes 524288
Async XLA Ops:
  0.7 0.7 %copy-start = (s32[1,1,1,9]{3,2,1,0:T(1,128)S(1)}, s32[1,1,1,9]{3,2,1,0:T(1,128)}, u32[]{:S(2)}) copy-start(s32[1,1,1,9]{3,2,1,0:T(1,128)} %off_hbm.1) | copy-start | bytes 112

commit v4 on v3

--- a/solution.py
+++ b/solution.py
@@ -10,21 +10,25 @@
 MESH = pl.DeviceIdType.MESH
 OWN, PAR, CRS = 0, 1, 2
 VMEM_LIMIT = 56164352
-D_SIZES = (4, 4, 8)
-P_SIZES = (8, 8)
-X_FIRST = ()
+D_SIZES = (4, 4, 4, 4)
+P_SIZES = (8, 4, 4)
+X_FIRST, Z_FAR, X_NEAR = ((2,), (0,), (0,))
 ORDER = {
     "S": (
-        0, 1, 2, 45, 46, 47, 48, 49, 50, 51, 52, 53, 3, 4, 6, 54, 55, 56, 57, 58, 59, 60, 61, 62, 63, 69,
-        17, 18, 20, 90, 73, 94, 8, 77, 98, 64, 85, 31, 32, 34, 65, 67, 86, 22, 5, 7, 11, 19, 21, 25, 88, 36,
-        33, 39, 71, 9, 14, 10, 80, 28, 66, 92, 23, 24, 101, 42, 35, 87, 75, 12, 13, 37, 82, 26, 27, 96, 106,
-        103, 40, 41, 15, 16, 107, 29, 38, 79, 43, 30, 100, 84, 81, 105, 44, 102, 83, 104, 108,
+        0, 1, 2, 3, 60, 61, 4, 5, 7, 62, 63, 64, 65, 66, 67, 68, 69, 70, 71, 72, 73, 74, 75, 76, 77, 78, 18,
+        19, 21, 84, 105, 126, 32, 33, 35, 88, 109, 130, 9, 92, 113, 134, 46, 47, 49, 79, 100, 121, 80, 23,
+        82, 101, 122, 81, 6, 8, 12, 103, 37, 20, 22, 26, 124, 51, 34, 36, 40, 10, 48, 50, 54, 86, 11, 102,
+        15, 107, 24, 95, 123, 29, 128, 25, 116, 13, 14, 43, 52, 137, 38, 39, 57, 90, 53, 27, 28, 111, 97,
+        41, 42, 118, 132, 139, 55, 56, 16, 17, 30, 142, 44, 94, 115, 136, 58, 31, 96, 144, 117, 143, 45,
+        138, 59, 98, 120, 119, 140, 145, 99, 141,
     ),
     "R": (
-        0, 1, 2, 45, 14, 46, 47, 48, 49, 50, 51, 52, 3, 4, 6, 28, 53, 54, 55, 56, 57, 58, 59, 60, 61, 62,
-        63, 17, 18, 20, 42, 11, 15, 64, 8, 85, 16, 31, 32, 34, 65, 86, 79, 100, 25, 29, 81, 5, 7, 102, 22,
-        30, 80, 101, 82, 68, 19, 21, 103, 39, 43, 89, 33, 44, 72, 66, 12, 36, 13, 93, 35, 87, 26, 9, 76, 27,
-        10, 97, 70, 40, 23, 91, 83, 24, 74, 41, 104, 95, 78, 37, 106, 99, 38, 107, 108, 84, 105,
+        0, 1, 2, 3, 60, 15, 61, 4, 5, 7, 29, 62, 63, 64, 65, 66, 67, 68, 69, 70, 71, 72, 73, 74, 43, 75, 76,
+        77, 78, 18, 19, 21, 57, 12, 32, 33, 35, 79, 100, 46, 47, 49, 121, 80, 9, 101, 26, 30, 122, 81, 31,
+        115, 136, 16, 17, 117, 138, 95, 116, 40, 44, 137, 83, 6, 8, 97, 118, 139, 45, 104, 20, 22, 23, 54,
+        58, 125, 13, 14, 59, 34, 36, 37, 27, 87, 48, 28, 108, 50, 102, 51, 41, 129, 123, 42, 91, 55, 112,
+        56, 133, 85, 106, 127, 10, 94, 11, 89, 110, 131, 96, 93, 38, 39, 24, 142, 114, 135, 25, 119, 98, 52,
+        140, 53, 143, 144, 145, 99, 120, 141,
     ),
 }
 
@@ -54,7 +58,7 @@
         self.role = role
 
 
-def make_tasks(d_sizes, p_sizes, x_first=()):
+def make_tasks(d_sizes, p_sizes, x_first=(), z_far=(), x_near=()):
     tasks = []
     for q in range(len(d_sizes)):
         c = slot(0, 1, OWN)
@@ -76,12 +80,10 @@
         ]))
         for dz in (0, 2):
             c = slot(0, dz, OWN)
-            tasks.append(Task("relay", q, [c], sends=[
-                (c, far(dz, PAR), "outer", "S"),
-                (c, slot(1, dz, OWN), "sib", None),
-            ]))
+            across = [] if q in z_far else [(c, far(dz, PAR), "outer", "S")]
+            tasks.append(Task("relay", q, [c], sends=across + [(c, slot(1, dz, OWN), "sib", None)]))
             c = slot(0, dz, PAR)
-            sends = [(c, far(dz, OWN), "outer", "S")]
+            sends = [] if q in z_far else [(c, far(dz, OWN), "outer", "S")]
             if q not in x_first:
                 sends.append((c, slot(0, dz, CRS), "xd", None))
             sends.append((c, slot(1, dz, PAR), "sib", None))
@@ -99,8 +101,8 @@
                 if dz == 1:
                     sends += [
                         (c, far(1, 1 - k), "partner", "R"),
-                        (c, far(0, k), "zp", "S"),
-                        (c, far(2, k), "zm", "S"),
+                        (c, far(0, k), "zp", None if q in z_far else "S"),
+                        (c, far(2, k), "zm", None if q in z_far else "S"),
                     ]
                 if k == PAR:
                     sends.append((c, slot(2, dz, CRS), "sxd", None))
@@ -120,10 +122,14 @@
     for q, size in enumerate(p_sizes):
         unit = 0.14 * size / 16
         for dz in (0, 2):
-            tasks.append(Task("add", q, [("RN", dz * 3 + CRS)], cost=unit, args=(("AX", dz), dz * 3 + CRS), sends=[
-                (("AX", dz), ("ZX", dz // 2), "zm" if dz == 0 else "zp", None)]))
-        tasks.append(Task("add", q, [("RN", 3 + CRS), ("ZX", 0), ("ZX", 1)], cost=unit * 1.5,
-                          args=(("AX", 1), 3 + CRS), sends=[(("AX", 1), ("XN", 0), "xp", None)]))
+            send = (("AX", dz), ("ZX", dz // 2), "zm" if dz == 0 else "zp", None)
+            if q in x_near:
+                send = (("AX", dz), ("XN", dz), "xp", None)
+            tasks.append(Task("add", q, [("RN", dz * 3 + CRS)], cost=unit, args=(("AX", dz), dz * 3 + CRS),
+                              sends=[send]))
+        waits = [("RN", 3 + CRS)] + ([] if q in x_near else [("ZX", 0), ("ZX", 1)])
+        tasks.append(Task("add", q, waits, cost=unit * 1.5,
+                          args=(("AX", 1), 3 + CRS), sends=[(("AX", 1), ("XN", 1), "xp", None)]))
         for dz in (0, 2, 1):
             for k in (PAR, OWN):
                 here = ("AF", dz * 2 + k)
@@ -138,10 +144,11 @@
                                   args=(here, None), sends=[(here, ("EN", dz * 2 + 1 - k), "outer", "R")]))
         for dz in (0, 2):
             for k in (PAR, OWN):
-                tasks.append(Task("add", q, [("RN", dz * 3 + k)], [("EN", dz * 2 + k)], cost=unit * 1.2,
+                waits = [("RN", dz * 3 + k)] + ([("XN", dz)] if k == PAR and q in x_near else [])
+                tasks.append(Task("add", q, waits, [("EN", dz * 2 + k)], cost=unit * 1.2,
                                   args=(("AZ", dz + k), dz * 3 + k), sends=[
                     (("AZ", dz + k), ("ZN", dz + k), "zm" if dz == 0 else "zp", None)]))
-        tasks.append(Task("add", q, [("RN", 3 + PAR), ("XN", 0), ("ZN", PAR), ("ZN", 2 + PAR)],
+        tasks.append(Task("add", q, [("RN", 3 + PAR), ("XN", 1), ("ZN", PAR), ("ZN", 2 + PAR)],
                           [("EN", 2 + PAR)], cost=unit * 1.6, args=(("AI", 0), 3 + PAR), sends=[
             (("AI", 0), ("IN", 0), "partner", None)]))
         tasks.append(Task("add", q, [("RN", 3 + OWN), ("ZN", OWN), ("ZN", 2 + OWN), ("IN", 0)],
@@ -156,7 +163,7 @@
 BUFFERS = {
     "H": (28, True), "F": (6, True),
     "O": (18, False), "AX": (3, False), "AF": (6, False), "AZ": (4, False), "AI": (1, False),
-    "RN": (9, False), "RF": (6, False), "XN": (1, False), "XF": (3, False), "ZX": (2, False),
+    "RN": (9, False), "RF": (6, False), "XN": (3, False), "XF": (3, False), "ZX": (2, False),
     "IF": (6, False), "EN": (6, False), "ZN": (4, False), "IN": (1, False),
 }
 
@@ -170,8 +177,10 @@
         return ("far", index if name == "RF" else index * 2 + PAR)
     if name == "ZX":
         return ("cross", 1)
-    if name in ("XN", "IN"):
-        return ("centre", PAR if name == "XN" else OWN)
+    if name == "XN":
+        return ("centre", PAR) if index == 1 else ("outside", index, PAR)
+    if name == "IN":
+        return ("centre", OWN)
     if name == "ZN":
         return ("centre", index % 2)
     dz, k = divmod(index, 3 if name == "RN" else 2)
@@ -334,7 +343,7 @@
             picked[s * size:(s + 1) * size] = halo[q][chosen[27 + s]]
         total[...] += jnp.dot(tiles[q][...], picked[:slots * size], preferred_element_type=jnp.float32)
 
-    tasks = make_tasks(D_SIZES, P_SIZES, X_FIRST)
+    tasks = make_tasks(D_SIZES, P_SIZES, X_FIRST, Z_FAR, X_NEAR)
 
     def send_number(straight, q, n):
         return (q if straight else len(D_SIZES) + q) * SEND_GROUPS + n // TOGETHER

time: 60.5 us -> 57.8 us (0.955)
  Pallas kernels: 58.3 us -> 55.7 us
    pallas_call x1, Pallas kernels: 58.3 us -> 55.7 us  [local(): pl.pallas_call(kernel, out_shape=jax.ShapeDtypeStruct(density.shape, dens...]
where the time goes in v4:
time: 57.8 us; the launch traced here: 57.7 us
  Pallas kernels  55.7 us (96%)
  local copies, waits for them, and re-layouts  1.35 us (2%)
  between operations  0.67 us (1%)
    pallas_call x1, Pallas kernels, local(): pl.pallas_call(kernel, out_shape=jax.ShapeDtypeStruct(density.shape, dens...  55.7 us
    unnamed x3, local copies, waits for them, and re-layouts  1.35 us

profile of v4, /device:TPU:1, one launch (start us, length us, event | category | flops | bytes accessed | tf_op | source)
XLA Modules:
  0.0 57.7 jit_solution(7325753899591858663)
XLA Ops:
  0.7 0.0 copy-start
  0.7 0.6 %copy-done = s32[1,1,1,9]{3,2,1,0:T(1,128)S(1)} copy-done((s32[1,1,1,9]{3,2,1,0:T(1,128)S(1)}, s32[1,1,1,9]{3,2,1,0:T(1,128)}, u32[]{:S(2)}) %copy-start) | copy-done | bytes 60
  1.3 55.7 %shard_map.46 = bf16[1,1,1,512,256]{4,3,2,1,0:T(8,128)(2,1)S(1)} custom-call(s32[1,1,1,9]{3,2,1,0:T(1,128)S(1)} %copy-done, s32[1,1,1]{2,1,0:T(1,128)S(6)} %copy.6.cnt_hbm, bf16[1,1,1,512,256]{4,3,2,1,0:T(8,128)(2,1)} %dens_ref.1, bf16[1,1,1,9,512,512]{5,4,3,2,1,0:T(8,128)(2,1)} %tile_hbm.1), custom_call_target="tpu_custom_call" | custom-call | tf_op jit(solution)/shard_map/pallas_call | solution.py:428
  57.0 0.7 %copy.7 = bf16[1,1,1,512,256]{4,3,2,1,0:T(8,128)(2,1)} copy(bf16[1,1,1,512,256]{4,3,2,1,0:T(8,128)(2,1)S(1)} %shard_map.46) | data formatting | bytes 524288
Async XLA Ops:
  0.7 0.7 %copy-start = (s32[1,1,1,9]{3,2,1,0:T(1,128)S(1)}, s32[1,1,1,9]{3,2,1,0:T(1,128)}, u32[]{:S(2)}) copy-start(s32[1,1,1,9]{3,2,1,0:T(1,128)} %off_hbm.1) | copy-start | bytes 112

commit v5 on v4

--- a/solution.py
+++ b/solution.py
@@ -158,7 +158,7 @@
     return tasks
 
 
-TOGETHER, SEND_GROUPS = 18, 4
+TOGETHER, SEND_GROUPS = 18, 3
 
 BUFFERS = {
     "H": (28, True), "F": (6, True),
@@ -171,10 +171,10 @@
 def group_of(name, index):
     if name == "H":
         return ("near", index) if index < 9 else ("sibling",)
-    if name in ("F", "IF"):
+    if name == "F":
         return (name, index)
-    if name in ("RF", "XF"):
-        return ("far", index if name == "RF" else index * 2 + PAR)
+    if name in ("RF", "XF", "IF"):
+        return ("far", index * 2 + PAR if name == "XF" else index)
     if name == "ZX":
         return ("cross", 1)
     if name == "XN":
@@ -191,7 +191,7 @@
 
 def arrivals_of():
     numbers = {}
-    for name in ("H", "F", "RN", "RF", "IF"):
+    for name in ("H", "F", "RN", "RF"):
         for index in range(BUFFERS[name][0]):
             for q in range(len(chunks_of(name))):
                 if name != "H" or index not in (3, 27):

time: 57.8 us -> 57.6 us (level)
  no operation moved by 1% of the time
where the time goes in v5:
time: 57.6 us; the launch traced here: 57.5 us
  Pallas kernels  55.4 us (96%)
  local copies, waits for them, and re-layouts  1.35 us (2%)
  between operations  0.67 us (1%)
    pallas_call x1, Pallas kernels, local(): pl.pallas_call(kernel, out_shape=jax.ShapeDtypeStruct(density.shape, dens...  55.4 us
    unnamed x3, local copies, waits for them, and re-layouts  1.35 us

profile of v5, /device:TPU:1, one launch (start us, length us, event | category | flops | bytes accessed | tf_op | source)
XLA Modules:
  0.0 57.5 jit_solution(2989390817131223983)
XLA Ops:
  0.7 0.0 copy-start
  0.7 0.6 %copy-done = s32[1,1,1,9]{3,2,1,0:T(1,128)S(1)} copy-done((s32[1,1,1,9]{3,2,1,0:T(1,128)S(1)}, s32[1,1,1,9]{3,2,1,0:T(1,128)}, u32[]{:S(2)}) %copy-start) | copy-done | bytes 60
  1.3 55.4 %shard_map.46 = bf16[1,1,1,512,256]{4,3,2,1,0:T(8,128)(2,1)S(1)} custom-call(s32[1,1,1,9]{3,2,1,0:T(1,128)S(1)} %copy-done, s32[1,1,1]{2,1,0:T(1,128)S(6)} %copy.6.cnt_hbm, bf16[1,1,1,512,256]{4,3,2,1,0:T(8,128)(2,1)} %dens_ref.1, bf16[1,1,1,9,512,512]{5,4,3,2,1,0:T(8,128)(2,1)} %tile_hbm.1), custom_call_target="tpu_custom_call" | custom-call | tf_op jit(solution)/shard_map/pallas_call | solution.py:428
  56.8 0.7 %copy.7 = bf16[1,1,1,512,256]{4,3,2,1,0:T(8,128)(2,1)} copy(bf16[1,1,1,512,256]{4,3,2,1,0:T(8,128)(2,1)S(1)} %shard_map.46) | data formatting | bytes 524288
Async XLA Ops:
  0.7 0.7 %copy-start = (s32[1,1,1,9]{3,2,1,0:T(1,128)S(1)}, s32[1,1,1,9]{3,2,1,0:T(1,128)}, u32[]{:S(2)}) copy-start(s32[1,1,1,9]{3,2,1,0:T(1,128)} %off_hbm.1) | copy-start | bytes 112
